TPU v7x, 32 devices: a whole 2x2x4 slice. The times are simulated.
32 devices in a mesh: data: 2 (over x), store: 4 (over z), model: 4 (over y, core).
Axes of the slice: x: 2, y: 2, z: 4, core: 2. Of those that a mesh axis runs over, the one named last changes fastest.
Arguments:
- queries: bfloat16 [512, 4096], P('data'), parts along dimension 0
- w_head: bfloat16 [4096, 32000], P(None, 'model')
- store_keys: bfloat16 [131072, 4096], P(('store', 'model'))
- store_tok: int32 [131072], P(('store', 'model'))
- temperature: float32 [], replicated
- mix_weight: float32 [], replicated
Outputs:
- output: float32 [512, 32000], P(('data', 'store'), 'model'), parts along dimension 0
There are 2 independent parts. A program takes and returns all parts, laid end to end along the dimension named above; an argument that names none is the same for every part.
All inputs are finite; a program needn't handle non-finite values.
Results may differ from a plain program's by a relative error of at most 0.001.
Values are sent between devices in bfloat16 or wider.
A program may use at most 1 GiB of HBM per device.

v0:
```python
import jax
import jax.numpy as jnp
from jax import lax
from jax.sharding import PartitionSpec as P


def solution(mesh):
    store_devs = mesh.shape["store"]
    model_devs = mesh.shape["model"]
    group_axes = ("store", "model")

    def local_step(queries, w_head, store_keys, store_tok, value_a11, mix_weight):
        vocab_loc = w_head.shape[1]
        rows_loc = queries.shape[0] // store_devs
        key_dots = lax.dot_general(store_keys, queries, (((1,), (1,)), ((), ())), preferred_element_type=jnp.float32)
        key_norms = jnp.sum(jnp.square(store_keys.astype(jnp.float32)), axis=1)
        scores = (2.0 * key_dots - key_norms[:, None]) / value_a11
        row_top = lax.pmax(jnp.max(scores, axis=0), group_axes)
        weights = jnp.exp(scores - row_top)
        row_total = lax.psum(jnp.sum(weights, axis=0), group_axes)
        histogram = jax.ops.segment_sum(weights, store_tok, num_segments=vocab_loc * model_devs)
        histogram = lax.psum_scatter(histogram, "model", scatter_dimension=0, tiled=True)
        histogram = lax.psum_scatter(histogram, "store", scatter_dimension=1, tiled=True)
        row_start = lax.axis_index("store") * rows_loc
        my_rows = lax.dynamic_slice_in_dim(queries, row_start, rows_loc, axis=0)
        my_total = lax.dynamic_slice_in_dim(row_total, row_start, rows_loc)
        logits = lax.dot_general(w_head, my_rows, (((0,), (1,)), ((), ())), preferred_element_type=jnp.float32)
        lm_top = lax.pmax(jnp.max(logits, axis=0), "model")
        lm_exp = jnp.exp(logits - lm_top)
        lm_total = lax.psum(jnp.sum(lm_exp, axis=0), "model")
        mixed = mix_weight * (histogram / my_total) + (1.0 - mix_weight) * (lm_exp / lm_total)
        return jnp.log(mixed).T

    return jax.shard_map(local_step, mesh=mesh, in_specs=(P("data", None), P(None, "model"), P(group_axes, None), P(group_axes), P(), P()), out_specs=P(("data", "store"), "model"), check_vma=False)
```

profile of v0, /device:TPU:0, one launch (start us, length us, event | category | flops | bytes accessed | tf_op | source)
XLA Modules:
  0.0 538.1 jit_solution(17693853591935106306)
XLA Ops:
  6.5 0.0 copy-start
  6.5 0.0 reduce-scatter.7.cloned.1.call-start
  6.5 21.0 %multiply_reduce_fusion = f32[8192]{0:T(1024)S(1)} fusion(bf16[8192,4096]{1,0:T(8,128)(2,1)} %param.8), kind=kLoop, calls=%fused_computation.1 | loop fusion | flops 100655104 | bytes 67141632 | tf_op jit(solution)/shard_map/reduce_sum | solution.py:16
  28.2 0.0 copy-done
  28.3 29.3 %fusion.12 = (f32[256]{0:T(256)S(1)}, f32[8192,256]{1,0:T(8,128)}) fusion(f32[]{:T(128)S(6)} %copy.11, f32[8192]{0:T(1024)S(1)} %multiply_reduce_fusion, bf16[8192,4096]{1,0:T(8,128)(2,1)} %param.8, bf16[256,4096]{1,0:T(8,128)(2,1)S(1)} %copy-done), kind=kOutput, calls=%fused_computation.18 | convolution fusion | flops 17188257792 | bytes 77628416 | tf_op jit(solution)/shard_map/dot_general | solution.py:15
  57.6 35.0 %pmax.14 = f32[256]{0:T(256)S(1)} all-reduce(f32[256]{0:T(256)S(1)} %get-tuple-element.5), channel_id=1, replica_groups=mesh['data'=2,'store'=4,'model'=4] {'store','model'}, use_global_device_ids=true, to_apply=%region_2.0 | all-reduce | flops 256 | bytes 2048 | tf_op jit(solution)/shard_map/pmax | solution.py:18
  92.5 58.7 %scatter_custom_fusion = f32[32000,256]{1,0:T(8,128)} fusion(s32[8192]{0:T(1024)} %param.9, f32[]{:T(128)} %constant.2.clone.1, f32[8192,256]{1,0:T(8,128)} %get-tuple-element.6, f32[256]{0:T(256)S(1)} %pmax.14), kind=kCustom, calls=%fused_computation.2 | custom fusion | flops 4194304 | bytes 41158144 | tf_op jit(solution)/shard_map/scatter-add | solution.py:21
  151.2 0.0 reduce-scatter.7.cloned.1.call-update
  151.2 0.0 reduce-scatter.5.cloned.1.call-start
  151.3 224.3 %reduce-scatter.7.cloned.1.call-done = f32[8000,256]{1,0:T(8,128)} async-done(((f32[32000,256]{1,0:T(8,128)}), f32[8000,256]{1,0:T(8,128)}) %reduce-scatter.7.cloned.1.call-update) | async-done | bytes 8192016
  375.6 8.9 %copy.10 = f32[8000,256]{0,1:T(8,128)} copy(f32[8000,256]{1,0:T(8,128)} %reduce-scatter.7.cloned.1.call-done) | data formatting | bytes 16384000
  384.5 0.0 reduce-scatter.5.cloned.1.call-update
  385.2 4.5 fusion.4
  389.7 32.7 %psum.14 = f32[256]{0:T(256)S(1)} all-reduce(f32[256]{0:T(256)S(1)} %fusion.4), channel_id=1, replica_groups=mesh['data'=2,'store'=4,'model'=4] {'store','model'}, use_global_device_ids=true, to_apply=%region_7.0 | all-reduce | flops 256 | bytes 2048 | tf_op jit(solution)/shard_map/psum | solution.py:20
  422.4 0.1 dynamic_slice.6
  422.5 28.7 %fusion.13 = (f32[64]{0:T(128)S(1)}, f32[64,8000]{1,0:T(8,128)}) fusion(bf16[4096,8000]{0,1:T(8,128)(2,1)} %param.7, bf16[256,4096]{1,0:T(8,128)(2,1)S(1)} %copy-done, s32[]{:T(128)S(6)} %select_n.4), kind=kOutput, calls=%fused_computation.19 | convolution fusion | flops 4194816000 | bytes 68108544 | tf_op jit(solution)/shard_map/dot_general | solution.py:27
  451.2 6.1 %pmax.15 = f32[64]{0:T(128)S(1)} all-reduce(f32[64]{0:T(128)S(1)} %get-tuple-element.7), channel_id=1, replica_groups=mesh['data'=2,'store'=4,'model'=4] {'model'}, use_global_device_ids=true, to_apply=%region_9.0 | all-reduce | flops 64 | bytes 512 | tf_op jit(solution)/shard_map/pmax | solution.py:28
  457.3 2.0 fusion.8
  459.3 6.1 %psum.15 = f32[64]{0:T(128)S(1)} all-reduce(f32[64]{0:T(128)S(1)} %fusion.8), channel_id=1, replica_groups=mesh['data'=2,'store'=4,'model'=4] {'model'}, use_global_device_ids=true, to_apply=%region_11.0 | all-reduce | flops 64 | bytes 512 | tf_op jit(solution)/shard_map/psum | solution.py:30
  465.4 61.7 %reduce-scatter.5.cloned.1.call-done = f32[8000,64]{0,1:T(8,128)} async-done(((f32[8000,256]{0,1:T(8,128)}), f32[8000,64]{0,1:T(8,128)}) %reduce-scatter.5.cloned.1.call-update) | async-done | bytes 2048016 | tf_op jit(solution)/shard_map/reduce_scatter | solution.py:23
  527.1 4.3 fusion.7
Async XLA Ops:
  6.5 21.7 %copy-start = (bf16[256,4096]{1,0:T(8,128)(2,1)S(1)}, bf16[256,4096]{1,0:T(8,128)(2,1)}, u32[]{:S(2)}) copy-start(bf16[256,4096]{1,0:T(8,128)(2,1)} %param.6) | copy-start | bytes 6291460
  6.5 369.0 %reduce-scatter.7.cloned.1.call-start = ((), (), s32[]{:S(2)}) async-start(), calls=%async_computation.3 | async-start | bytes 40960000
  151.2 375.8 %reduce-scatter.5.cloned.1.call-start = ((), (), s32[]{:S(2)}) async-start(), calls=%async_computation.2 | async-start | bytes 10321920 | tf_op jit(solution)/shard_map/reduce_scatter | solution.py:23
Sparse Core Ops, SparseCore 0:
  151.4 224.1 reduce-scatter.6
  384.6 142.3 reduce-scatter.4
where the time goes:
time: 539 us; the launch traced here: 538 us
  waiting for transfers between devices  286 us (53%)
  other arithmetic  90.6 us (17%)
  blocking collectives  79.8 us (15%)
  matrix products  58.1 us (11%)
  between operations  14.7 us (3%)
  local copies, waits for them, and re-layouts  8.99 us (2%)
    unnamed x3, waiting for transfers between devices  224 us
    reduce_scatter x1, waiting for transfers between devices, local_step(): lax.psum_scatter(histogram, 'store', scatter_dimension=1, tiled=True)  61.7 us
    scatter-add x1, other arithmetic, local_step(): jax.ops.segment_sum(weights, store_tok, num_segments=vocab_loc * model_devs)  58.7 us
    pmax x1, blocking collectives, local_step(): row_top = lax.pmax(jnp.max(scores, axis=0), group_axes)  35 us
    psum x1, blocking collectives, local_step(): row_total = lax.psum(jnp.sum(weights, axis=0), group_axes)  32.7 us
    dot_general x1, matrix products, local_step(): lax.dot_general(store_keys, queries, (((1,), (1,)), ((), ())), preferred_...  29.3 us
    dot_general x1, matrix products, local_step(): lax.dot_general(w_head, my_rows, (((0,), (1,)), ((), ())), preferred_elem...  28.7 us
    reduce_sum x1, other arithmetic, local_step(): key_norms = jnp.sum(jnp.square(store_keys.astype(jnp.float32)), axis=1)  21 us
  transfers between devices with their start and end apart: 2, of which 2 were waited for; matrix products, arithmetic and copies ran while one was open for 7% of the time, Pallas kernels for 0%

commit v1 on v0

v1 whole, which is shorter than its diff:
```python
import functools

import jax
import jax.numpy as jnp
from jax import lax
from jax.experimental import pallas as pl
from jax.experimental.pallas import tpu as pltpu
from jax.sharding import PartitionSpec as P


LANES = 128
BLOCK = 512
BATCH = 16
VOCAB_LOC = 8000
PIECE = 4096
FIRST = 4
META = 8
SLOTS = 4
SCATTER_VMEM = 30 * 1024 * 1024
STEP = 976
UPPER = VOCAB_LOC - PIECE
FLAG = 1 << 16
CLASH = 1 << 17


def targets(me):
    left = me < 2
    return me, me ^ 1, jnp.where(left, 2, 1), jnp.where(left, 3, 0)


def scores_kernel(first, count, s_ref, tau_ref, q_ref, k_hbm, own_ref, near_ref, sparse_ref, dense_ref, qs_ref, held, sem):
    def fetch(block):
        slot = lax.rem(block, SLOTS)
        rows = pl.ds(pl.multiple_of((first + block) * BLOCK, BLOCK), BLOCK)
        return pltpu.make_async_copy(k_hbm.at[rows], held.at[slot], sem.at[slot])

    for block in range(SLOTS - 1):
        fetch(block).start()
    for k, z in enumerate(targets(s_ref[0])):
        qs_ref[64 * k:64 * k + 64, :] = q_ref[pl.ds(pl.multiple_of(z * 64, 64), 64), :]
    half = BLOCK // 2
    low = lax.broadcasted_iota(jnp.int32, (half, LANES), 1) < 64

    @pl.loop(0, count)
    def _(block):
        @pl.when(block + SLOTS - 1 < count)
        def _():
            fetch(block + SLOTS - 1).start()

        fetch(block).wait()
        keys = held[lax.rem(block, SLOTS)]
        dots = lax.dot_general(keys, qs_ref[...], (((1,), (1,)), ((), ())), preferred_element_type=jnp.float32)
        wide = keys.astype(jnp.float32)
        norms = jnp.sum(wide * wide, axis=1, keepdims=True)
        scores = (2.0 * dots - norms) / tau_ref[0]
        out = pl.ds(pl.multiple_of(block * half, half), half)
        for k, ref in enumerate((own_ref, near_ref, sparse_ref, dense_ref)):
            tile = scores[:, LANES * (k // 2):LANES * (k // 2) + LANES]
            top, bottom = tile[:half], tile[half:]
            if k % 2 == 0:
                ref[out, :] = jnp.where(low, top, pltpu.roll(bottom, 64, 1))
            else:
                ref[out, :] = jnp.where(low, pltpu.roll(top, 64, 1), bottom)


def score_call(me, tau, queries, keys, first, count):
    width = keys.shape[1]
    packed = jax.ShapeDtypeStruct((count * BLOCK // 2, LANES), jnp.float32)
    smem = pl.BlockSpec(memory_space=pltpu.SMEM)
    vmem = pl.BlockSpec(memory_space=pltpu.VMEM)
    return pl.pallas_call(
        functools.partial(scores_kernel, first, count),
        in_specs=[smem, smem, vmem, pl.BlockSpec(memory_space=pl.ANY)],
        out_specs=[vmem] * 4,
        out_shape=[packed] * 4,
        scratch_shapes=[pltpu.VMEM(queries.shape, queries.dtype), pltpu.VMEM((SLOTS, BLOCK, width), keys.dtype), pltpu.SemaphoreType.DMA((SLOTS,))],
        compiler_params=pltpu.CompilerParams(vmem_limit_bytes=30 * 1024 * 1024),
        cost_estimate=pl.CostEstimate(flops=2 * count * BLOCK * width * 256, bytes_accessed=count * BLOCK * width * 2, transcendentals=0),
        name="scores",
    )(me, tau, queries, keys)


def codes_kernel(m_ref, *refs):
    me = m_ref[0]
    for tok_ref, code_ref in zip(refs[:len(refs) // 2], refs[len(refs) // 2:]):
        tok = tok_ref[...]
        owner = sum((tok >= VOCAB_LOC * i).astype(jnp.int32) for i in (1, 2, 3))
        code = tok - owner * VOCAB_LOC + (owner ^ me) * VOCAB_LOC
        lane = lax.broadcasted_iota(jnp.int32, code.shape, 1)
        place = lane % BATCH
        clash = jnp.zeros_like(code)
        for d in range(1, BATCH):
            same = (code == pltpu.roll(code, LANES - d, 1)) & (place < BATCH - d)
            clash = clash | same.astype(jnp.int32)
        d = BATCH // 2
        while d:
            clash = clash | pltpu.roll(clash, LANES - d, 1)
            d //= 2
        any_clash = jnp.max(jnp.where(place == 0, clash, 0), axis=1, keepdims=True)
        code_ref[...] = code + jnp.where(place == 0, clash * CLASH, 0) * any_clash + jnp.where(place == 0, any_clash * FLAG, 0)


def codes_call(me, toks):
    shape = jax.ShapeDtypeStruct(toks[0].shape, jnp.int32)
    return pl.pallas_call(
        codes_kernel,
        in_specs=[pl.BlockSpec(memory_space=pltpu.SMEM)] + [pl.BlockSpec(memory_space=pltpu.VMEM)] * len(toks),
        out_specs=[pl.BlockSpec(memory_space=pltpu.VMEM)] * len(toks),
        out_shape=[shape] * len(toks),
        cost_estimate=pl.CostEstimate(flops=4_000_000, bytes_accessed=1 << 18, transcendentals=0),
        name="codes",
    )(me, *toks)


def fold(row, op):
    wide = jnp.broadcast_to(row, (8, LANES))
    return op(wide, pltpu.roll(wide, 64, 1))[:1]


def scatter_kernel(segments, n_codes, chunks, carried, s_ref, *refs):
    n_x = len(segments)
    code_refs, refs = refs[:n_codes], refs[n_codes:]
    x_refs, refs = refs[:n_x], refs[n_x:]
    if carried:
        prev_refs, refs = refs[:4], refs[4:]
    piece_refs = refs[:4]
    hist, e_ref, z_ref = refs[4:7]
    half = BLOCK // 2

    @pl.loop(0, hist.shape[0] // 320)
    def _(i):
        hist[pl.ds(pl.multiple_of(i * 320, 320), 320), :] = jnp.zeros((320, LANES), jnp.float32)

    z_ref[...] = jnp.zeros_like(z_ref)
    middle = (s_ref[0] == 1) | (s_ref[0] == 2)
    counts = [jnp.where(middle, x.shape[0] // half, 0) if seg[2] else x.shape[0] // half for x, seg in zip(x_refs, segments)]
    peak = jnp.full((8, LANES), -jnp.inf, jnp.float32)
    for x_ref, count in zip(x_refs, counts):
        def widen(block, peak):
            x = x_ref[pl.ds(pl.multiple_of(block * half, half), half), :]
            return jnp.maximum(peak, jnp.max(x.reshape(half // 8, 8, LANES), axis=0))

        peak = lax.fori_loop(0, count, widen, peak)
    top = fold(jnp.max(peak, axis=0, keepdims=True), jnp.maximum)

    for x_ref, (which, base, _), count in zip(x_refs, segments, counts):
        code_ref = code_refs[which]

        @pl.loop(0, count)
        def _(block):
            e = jnp.exp(x_ref[pl.ds(pl.multiple_of(block * half, half), half), :] - top)
            z_ref[...] += jnp.sum(e.reshape(half // 8, 8, LANES), axis=0)
            e_ref[:half] = e
            e_ref[half:] = pltpu.roll(e, 64, 1)

            @pl.loop(0, BLOCK // LANES)
            def _(group):
                row = pl.multiple_of(group * LANES, LANES)
                at = pl.multiple_of(base + block * BLOCK + group * LANES, LANES)
                ids_ref = code_ref.at[pl.ds(at, LANES)]
                rows_ref = e_ref.at[pl.ds(row, LANES)]
                head = ids_ref[0]

                @pl.when(head < FLAG)
                def _():
                    for b in range(0, LANES, BATCH):
                        ids = [ids_ref[b + i] for i in range(BATCH)]
                        new = [hist[pl.ds(ids[i], 1), :] + rows_ref[b + i:b + i + 1, :] for i in range(BATCH)]
                        for i in range(BATCH):
                            hist[pl.ds(ids[i], 1), :] = new[i]

                @pl.when(head >= FLAG)
                def _():
                    @pl.loop(0, LANES // BATCH)
                    def _(b):
                        mark = ids_ref[b * BATCH]
                        ids = [mark & (FLAG - 1)] + [ids_ref[b * BATCH + i] for i in range(1, BATCH)]
                        rows = rows_ref.at[pl.ds(pl.multiple_of(b * BATCH, BATCH), BATCH)]

                        @pl.when((mark & CLASH) == 0)
                        def _():
                            new = [hist[pl.ds(ids[i], 1), :] + rows[i:i + 1, :] for i in range(BATCH)]
                            for i in range(BATCH):
                                hist[pl.ds(ids[i], 1), :] = new[i]

                        @pl.when((mark & CLASH) != 0)
                        def _():
                            for i in range(BATCH):
                                hist[pl.ds(ids[i], 1), :] += rows[i:i + 1, :]

    z = fold(jnp.sum(z_ref[...], axis=0, keepdims=True), jnp.add)
    scale = held_scale = None
    if carried:
        held_top = prev_refs[0][PIECE + 1:PIECE + 2, :]
        both = jnp.maximum(top, held_top)
        scale, held_scale = jnp.exp(top - both), jnp.exp(held_top - both)
        z = z * scale + prev_refs[0][PIECE:PIECE + 1, :] * held_scale
        top = both
    meta = jnp.concatenate([z, top, jnp.zeros((META - 2, LANES), jnp.float32)], axis=0)
    size = PIECE // chunks

    def place(rel, c, at, rows, both):
        first = c * size + at
        lower = hist[pl.ds(pl.multiple_of(rel * VOCAB_LOC + first, 8), rows), :]
        low = lax.broadcasted_iota(jnp.int32, (rows, LANES), 1) < 64
        if both:
            value = jnp.where(low, lower, pltpu.roll(hist[pl.ds(pl.multiple_of(rel * VOCAB_LOC + PIECE + first, 8), rows), :], 64, 1))
        else:
            value = jnp.where(low, lower, 0.0)
        if carried:
            value = value * scale + prev_refs[rel][pl.ds(pl.multiple_of(first, 8), rows), :] * held_scale
        piece_refs[rel][pl.ds(pl.multiple_of(c * (size + META) + at, 8), rows), :] = value

    for rel in (3, 1, 2, 0):
        for c in range(chunks):
            full = min(size, UPPER - c * size)

            @pl.loop(0, full // STEP)
            def _(i):
                place(rel, c, i * STEP, STEP, True)

            rest = full % STEP
            if rest:
                place(rel, c, full - rest, rest, True)
            if full < size:
                place(rel, c, full, size - full, False)
            at = c * (size + META) + size
            piece_refs[rel][at:at + META, :] = meta


def scatter_call(s1, codes, xs, segments, prev, chunks):
    n_codes = len(codes)
    carried = prev is not None
    vmem = pl.BlockSpec(memory_space=pltpu.VMEM)
    smem = pl.BlockSpec(memory_space=pltpu.SMEM)
    piece = jax.ShapeDtypeStruct((PIECE + chunks * META, LANES), jnp.float32)
    n_keys = sum(2 * x.shape[0] for x in xs)
    return pl.pallas_call(
        functools.partial(scatter_kernel, segments, n_codes, chunks, carried),
        in_specs=[smem] + [smem] * n_codes + [vmem] * len(xs) + ([vmem] * 4 if carried else []),
        out_specs=[vmem] * 4,
        out_shape=[piece] * 4,
        scratch_shapes=[pltpu.VMEM((4 * VOCAB_LOC, LANES), jnp.float32), pltpu.VMEM((BLOCK, LANES), jnp.float32), pltpu.VMEM((8, LANES), jnp.float32)],
        compiler_params=pltpu.CompilerParams(vmem_limit_bytes=SCATTER_VMEM),
        cost_estimate=pl.CostEstimate(flops=n_keys * 1_000_000, bytes_accessed=n_keys * 512, transcendentals=n_keys * 64),
        name="scatter",
    )(s1, *codes, *xs, *(prev if carried else ()))


def merge_kernel(size, offsets, *refs):
    out_ref = refs[-1]
    tops = [r[o + size + 1:o + size + 2, :] for r, o in zip(refs, offsets)]
    top = functools.reduce(jnp.maximum, tops)
    scales = [jnp.exp(t - top) for t in tops]

    def total(at, count):
        parts = [r[pl.ds(pl.multiple_of(o + at, 8), count), :] * f for r, o, f in zip(refs, offsets, scales)]
        return functools.reduce(jnp.add, parts)

    @pl.loop(0, size // 256)
    def _(i):
        out_ref[pl.ds(pl.multiple_of(i * 256, 256), 256), :] = total(i * 256, 256)

    rest = total(size, META)
    out_ref[size:size + META, :] = jnp.where(lax.broadcasted_iota(jnp.int32, (META, LANES), 0) == 1, top, rest)


def merge_call(size, parts):
    vmem = pl.BlockSpec(memory_space=pltpu.VMEM)
    return pl.pallas_call(
        functools.partial(merge_kernel, size, tuple(c * (size + META) for _, c in parts)),
        in_specs=[vmem] * len(parts),
        out_specs=vmem,
        out_shape=jax.ShapeDtypeStruct((size + META, LANES), jnp.float32),
        compiler_params=pltpu.CompilerParams(vmem_limit_bytes=24 * 1024 * 1024),
        cost_estimate=pl.CostEstimate(flops=4_000_000_000, bytes_accessed=size * 2048, transcendentals=0),
        name="merge",
    )(*[a for a, _ in parts])


def final_kernel(chunks, s_ref, mix_ref, logits_ref, s0_ref, s1_ref, s2_ref, s3_ref, keep_ref, mate_ref, fromy_ref, *refs):
    far_refs, out_ref = refs[:chunks], refs[chunks]
    mix = mix_ref[0]
    end = (s_ref[0] == 0) | (s_ref[0] == 3)
    size = PIECE // chunks
    whole = (keep_ref, mate_ref, fromy_ref)
    metas = [r[PIECE:PIECE + META, :] for r in whole] + [far_refs[0][size:size + META, :]]
    tops = [t[1:2] for t in metas]
    tops[3] = jnp.where(end, tops[3], -jnp.inf)
    top = functools.reduce(jnp.maximum, tops)
    scales = [jnp.exp(t - top) for t in tops]
    z = sum(t[0:1] * f for t, f in zip(metas, scales))
    scales = [f * (mix / z) for f in scales]
    stats = [r[...] for r in (s0_ref, s1_ref, s2_ref, s3_ref)]
    lm_top = functools.reduce(jnp.maximum, [t[:, :1] for t in stats])
    total = sum(t[:, 64:65] * jnp.exp(t[:, :1] - lm_top) for t in stats)
    lm_scale = (1.0 - mix) / total

    def lm(at, count):
        return jnp.exp(logits_ref[:, at:at + count] - lm_top) * lm_scale

    for i in range(0, PIECE, LANES):
        far = far_refs[i // size][i % size:i % size + LANES, :]
        h = sum(r[i:i + LANES, :] * f for r, f in zip(whole, scales)) + far * scales[3]
        h = h.T
        out_ref[:, i:i + LANES] = jnp.log(h[:64] + lm(i, LANES))
        count = min(LANES, UPPER - i)
        if count > 0:
            out_ref[:, PIECE + i:PIECE + i + count] = jnp.log(h[64:, :count] + lm(PIECE + i, count))


def final_call(s1, mix, logits, stats, whole, far):
    vmem = pl.BlockSpec(memory_space=pltpu.VMEM)
    smem = pl.BlockSpec(memory_space=pltpu.SMEM)
    return pl.pallas_call(
        functools.partial(final_kernel, len(far)),
        in_specs=[smem, smem] + [vmem] * (8 + len(far)),
        out_specs=vmem,
        out_shape=jax.ShapeDtypeStruct(logits.shape, jnp.float32),
        compiler_params=pltpu.CompilerParams(vmem_limit_bytes=40 * 1024 * 1024),
        cost_estimate=pl.CostEstimate(flops=5_000_000_000, bytes_accessed=12 << 20, transcendentals=1 << 20),
        name="final",
    )(s1, mix, logits, *stats, *whole, *far)


NEAR = [(0, 1), (1, 0), (2, 3), (3, 2)]
FAR2 = [(0, 2), (3, 1)]
FAR1 = [(1, 2), (2, 1)]
INWARD = [(0, 1), (3, 2)]
ACROSS = [(1, 3), (2, 0)]
CHUNKS = 2


def solution(mesh):
    store_devs = mesh.shape["store"]

    def swap(x, axis, bit):
        return lax.ppermute(x, axis, [(i, i ^ bit) for i in range(4)])

    def local_step(queries, w_head, store_keys, store_tok, temperature, mix_weight):
        rows_loc = queries.shape[0] // store_devs
        s = lax.axis_index("store")
        m = lax.axis_index("model")
        s1, m1 = s.reshape(1), m.reshape(1)
        tau = temperature.reshape(1)
        blocks = store_keys.shape[0] // BLOCK
        n_a = FIRST * BLOCK
        size = PIECE // CHUNKS
        tok2 = store_tok.reshape(-1, LANES)

        toks = [lax.ppermute(tok2, "store", NEAR), lax.ppermute(tok2, "store", FAR2), lax.ppermute(tok2, "store", FAR1)]
        own_a, near_a, sparse_a, dense_a = score_call(s1, tau, queries, store_keys, 0, FIRST)
        far2_a = lax.ppermute(sparse_a, "store", FAR2)
        far1_a = lax.ppermute(sparse_a, "store", FAR1)
        got_a = lax.ppermute(near_a, "store", NEAR)
        own_b, near_b, sparse_b, dense_b = score_call(s1, tau, queries, store_keys, FIRST, blocks - FIRST)
        far2_b = lax.ppermute(sparse_b, "store", FAR2)
        far1_b = lax.ppermute(sparse_b, "store", FAR1)
        got_b = lax.ppermute(near_b, "store", NEAR)
        code_own, code_near, code_far2, code_far1 = [c.reshape(-1) for c in codes_call(m1, [tok2] + toks)]

        dense = scatter_call(s1, [code_own], [dense_a, dense_b], ((0, 0, False), (0, n_a, False)), None, CHUNKS)
        d_next = swap(dense[3], "model", 1)
        d_mate = swap(dense[1], "model", 1)
        d_y = []
        for c in range(CHUNKS):
            part = merge_call(size, [(dense[2], c), (d_next, c)])
            d_y.append(swap(part, "model", 2))

        xs = [own_a, own_b, got_a, far2_a, far1_a]
        segments = ((0, 0, False), (0, n_a, False), (1, 0, False), (2, 0, True), (3, 0, True))
        part = scatter_call(s1, [code_own, code_near, code_far2, code_far1], xs, segments, None, 1)
        xs = [got_b, far2_b, far1_b]
        segments = ((0, n_a, False), (1, n_a, True), (2, n_a, True))
        keep, mate, ynext, matey = scatter_call(s1, [code_near, code_far2, code_far1], xs, segments, part, 1)
        matey = swap(matey, "model", 1)
        mate = swap(mate, "model", 1)

        far = []
        for c in range(CHUNKS):
            plane = merge_call(size, [(dense[0], c), (d_mate, c), (d_y[c], 0)])
            inward = lax.ppermute(plane, "store", INWARD)
            pair = merge_call(size, [(plane, 0), (inward, 0)])
            far.append(lax.ppermute(pair, "store", ACROSS))

        ynext = merge_call(PIECE, [(ynext, 0), (matey, 0)])
        from_y = swap(ynext, "model", 2)

        my_rows = lax.dynamic_slice_in_dim(queries, s * rows_loc, rows_loc, axis=0)
        logits = lax.dot_general(my_rows, w_head, (((1,), (0,)), ((), ())), preferred_element_type=jnp.float32)
        lm_top = jnp.max(logits, axis=1, keepdims=True)
        lm_sum = jnp.sum(jnp.exp(logits - lm_top), axis=1, keepdims=True)
        stats = jnp.concatenate([jnp.broadcast_to(lm_top, (rows_loc, 64)), jnp.broadcast_to(lm_sum, (rows_loc, 64))], axis=1)
        stats = [stats] + [swap(stats, "model", k) for k in (1, 2, 3)]
        return final_call(s1, mix_weight.reshape(1), logits, stats, [keep, mate, from_y], far)

    return jax.shard_map(local_step, mesh=mesh, in_specs=(P("data", None), P(None, "model"), P(("store", "model"), None), P(("store", "model")), P(), P()), out_specs=P(("data", "store"), "model"), check_vma=False)
```

time: 539 us -> 311 us (0.58)
  waiting for transfers between devices: 286 us -> 55.9 us
  Pallas kernels: 0 us -> 111 us
  other arithmetic: 90.6 us -> 0.58 us
  starting transfers between devices: 0.04 us -> 83.6 us
  blocking collectives: 79.8 us -> 0 us
  matrix products: 58.1 us -> 27.4 us
  local copies, waits for them, and re-layouts: 8.99 us -> 29.6 us
  between operations: 14.7 us -> 1.59 us
    unnamed x3 -> x0, waiting for transfers between devices: 224 us -> none
    pallas_call x0 -> x14, Pallas kernels: none -> 111 us  [the longest x3 63 us: scatter_call(): pl.pallas_call(functools.partial(scatter_kernel, segments, n_codes, chunk...]
    ppermute x0 -> x23, starting transfers between devices: none -> 83.6 us  [the longest x2 54 us: local_step(): inward = lax.ppermute(plane, 'store', INWARD)]
    reduce_scatter x1 -> x0, waiting for transfers between devices: 61.7 us -> none  [local_step(): lax.psum_scatter(histogram, 'store', scatter_dimension=1, tiled=True)]
    scatter-add x1 -> x0, other arithmetic: 58.7 us -> none  [local_step(): jax.ops.segment_sum(weights, store_tok, num_segments=vocab_loc * model_devs)]
    ppermute x0 -> x23, waiting for transfers between devices: none -> 55.9 us  [the longest x10 29.3 us: swap(): return lax.ppermute(x, axis, [(i, i ^ bit) for i in range(4)])]
    pmax x2 -> x0, blocking collectives: 41 us -> none  [the longest x1 35 us: local_step(): row_top = lax.pmax(jnp.max(scores, axis=0), group_axes)]
    psum x2 -> x0, blocking collectives: 38.7 us -> none  [the longest x1 32.7 us: local_step(): row_total = lax.psum(jnp.sum(weights, axis=0), group_axes)]
  transfers between devices with their start and end apart: 2 -> 23, of which waited for: 2 -> 7; matrix products, arithmetic and copies ran while one was open for 7% -> 9% of each run, Pallas kernels for 0% -> 34%
where the time goes in v1:
time: 311 us; the launch traced here: 310 us
  Pallas kernels  111 us (36%)
  starting transfers between devices  83.6 us (27%)
  waiting for transfers between devices  55.9 us (18%)
  local copies, waits for them, and re-layouts  29.6 us (10%)
  matrix products  27.4 us (9%)
    pallas_call x3, Pallas kernels, scatter_call(): pl.pallas_call(functools.partial(scatter_kernel, segments, n_codes, chunk...  63 us
    ppermute x2, starting transfers between devices, local_step(): inward = lax.ppermute(plane, 'store', INWARD)  54 us
    unnamed x66, local copies, waits for them, and re-layouts  29.5 us
    pallas_call x2, Pallas kernels, score_call(): pl.pallas_call(functools.partial(scores_kernel, first, count), in_specs=[...  29.5 us
    ppermute x10, waiting for transfers between devices, swap(): return lax.ppermute(x, axis, [(i, i ^ bit) for i in range(4)])  29.3 us
    dot_general x1, matrix products, local_step(): lax.dot_general(my_rows, w_head, (((1,), (0,)), ((), ())), preferred_elem...  27.4 us
    ppermute x1, waiting for transfers between devices, local_step(): got_a = lax.ppermute(near_a, 'store', NEAR)  13.8 us
    ppermute x2, waiting for transfers between devices, local_step(): inward = lax.ppermute(plane, 'store', INWARD)  11.5 us
  transfers between devices with their start and end apart: 23, of which 7 were waited for; matrix products, arithmetic and copies ran while one was open for 9% of the time, Pallas kernels for 34%

profile of v1, /device:TPU:0, one launch (start us, length us, event | category | flops | bytes accessed | tf_op | source)
XLA Modules:
  0.0 309.6 jit_solution(281427559580163433)
XLA Ops:
  0.0 3.1 collective-permute-start.3
  3.1 4.5 %collective-permute-start.4 = (s32[64,128]{1,0:T(8,128)}, s32[64,128]{1,0:T(8,128)S(1)}, u32[]{:S(2)}, u32[]{:S(2)}) collective-permute-start(s32[64,128]{1,0:T(8,128)} %bitcast.22), channel_id=1, source_target_pairs={{0,8},{12,4},{1,9},{13,5},{2,10},{14,6},{3,11},{15,7},{16,24},{28,... | collective-permute-start | bytes 98312 | tf_op jit(solution)/shard_map/ppermute | solution.py:351
  8.9 1.6 copy-done
  10.5 9.1 %scores.3 = (f32[1024,128]{1,0:T(8,128)S(1)}, f32[1024,128]{1,0:T(8,128)S(1)}, f32[1024,128]{1,0:T(8,128)}, f32[1024,128]{1,0:T(8,128)S(1)}) custom-call(s32[1]{0:T(128)} %bitcast.s_ref, f32[1]{0:T(128)} %bitcast.11.tau_ref, bf16[256,4096]{1,0:T(8,128)(2,1)S(1)} %copy-done, bf16[8192,4096]{1,0:T(8,128)(2,1)} %k_hbm.3), custom_call_target="tpu_custom_call" | custom-call | flops 4294967296 | bytes 16777216 | tf_op jit(solution)/shard_map/scores/pallas_call | solution.py:71
  21.9 3.3 %collective-permute-start.10 = (f32[1024,128]{1,0:T(8,128)}, f32[1024,128]{1,0:T(8,128)}, u32[]{:S(2)}, u32[]{:S(2)}) collective-permute-start(f32[1024,128]{1,0:T(8,128)} %get-tuple-element.38), channel_id=1, source_target_pairs={{0,8},{12,4},{1,9},{13,5},{2,10},{14,6},{3,11},{15,7},{16,24},{28,... | collective-permute-start | bytes 1572872 | tf_op jit(solution)/shard_map/ppermute | solution.py:353
  25.3 1.5 collective-permute-start.11
  26.7 20.4 %scores.2 = (f32[3072,128]{1,0:T(8,128)S(1)}, f32[3072,128]{1,0:T(8,128)S(1)}, f32[3072,128]{1,0:T(8,128)S(1)}, f32[3072,128]{1,0:T(8,128)S(1)}) custom-call(s32[1]{0:T(128)} %bitcast.s_ref, f32[1]{0:T(128)} %bitcast.10.tau_ref, bf16[256,4096]{1,0:T(8,128)(2,1)S(1)} %copy-done, bf16[8192,4096]{1,0:T(8,128)(2,1)} %k_hbm.3), custom_call_target="tpu_custom_call" | custom-call | flops 12884901888 | bytes 50331648 | tf_op jit(solution)/shard_map/scores/pallas_call | solution.py:71
  49.4 4.2 %collective-permute-start.7 = (f32[3072,128]{1,0:T(8,128)S(1)}, f32[3072,128]{1,0:T(8,128)}, u32[]{:S(2)}, u32[]{:S(2)}) collective-permute-start(f32[3072,128]{1,0:T(8,128)S(1)} %get-tuple-element.33), channel_id=1, source_target_pairs={{0,8},{12,4},{1,9},{13,5},{2,10},{14,6},{3,11},{15,7},{16,24},{28,... | collective-permute-start | bytes 4718600 | tf_op jit(solution)/shard_map/ppermute | solution.py:357
  53.6 1.8 collective-permute-start.8
  56.0 3.3 %codes.1 = (s32[64,128]{1,0:T(8,128)}, s32[64,128]{1,0:T(8,128)}, s32[64,128]{1,0:T(8,128)}, s32[64,128]{1,0:T(8,128)}) custom-call(s32[1]{0:T(128)} %bitcast.2.m_ref, s32[64,128]{1,0:T(8,128)} %bitcast.24, s32[64,128]{1,0:T(8,128)} %copy-done.30, s32[64,128]{1,0:T(8,128)} %copy-done.31, s32[64,128]{1,0:T(8,128)} %copy-done.32), custom_call_target="tpu_custom_call" | custom-call | flops 4000000 | bytes 262144 | tf_op jit(solution)/shard_map/codes/pallas_call | solution.py:105
  59.3 1.4 collective-permute-start.6
  60.8 1.4 copy-done.4
  64.0 19.4 %scatter.5 = (f32[4112,128]{1,0:T(8,128)S(1)}, f32[4112,128]{1,0:T(8,128)S(1)}, f32[4112,128]{1,0:T(8,128)S(1)}, f32[4112,128]{1,0:T(8,128)S(1)}) custom-call(s32[1]{0:T(128)} %bitcast.s_ref, s32[8192]{0:T(1024)S(1)} %bitcast.19, f32[1024,128]{1,0:T(8,128)S(1)} %copy-done.9, f32[3072,128]{1,0:T(8,128)S(1)} %copy-done.4), custom_call_target="tpu_custom_call" | custom-call | flops 8192000000 | bytes 4194304 | tf_op jit(solution)/shard_map/scatter/pallas_call | solution.py:238
  83.4 1.3 copy-done.19
  84.8 13.8 %collective-permute-done.9.refs_6_ = f32[1024,128]{1,0:T(8,128)} collective-permute-done((f32[1024,128]{1,0:T(8,128)}, f32[1024,128]{1,0:T(8,128)}, u32[]{:S(2)}, u32[]{:S(2)}) %collective-permute-start.9) | collective-permute-done | bytes 524320 | tf_op jit(solution)/shard_map/ppermute | solution.py:355
  98.6 24.8 %scatter.3 = (f32[4104,128]{1,0:T(8,128)S(1)}, f32[4104,128]{1,0:T(8,128)S(1)}, f32[4104,128]{1,0:T(8,128)S(1)}, f32[4104,128]{1,0:T(8,128)S(1)}) custom-call(s32[1]{0:T(128)} %bitcast.s_ref, s32[8192]{0:T(1024)S(1)} %bitcast.20, s32[8192]{0:T(1024)S(1)} %bitcast.13, s32[8192]{0:T(1024)S(1)} %bitcast.15, s32[8192]{0:T(1024)S(1)} %bitcast.17, ...), custom_call_target="tpu_custom_call" | custom-call | flops 14336000000 | bytes 7340032 | tf_op jit(solution)/shard_map/scatter/pallas_call | solution.py:238
  123.5 1.4 copy-done.22
  124.8 1.3 copy-done.24
  126.2 1.4 copy-done.26
  127.5 1.3 copy-done.28
  128.8 1.3 collective-permute-done.6.refs_3_
  130.2 1.6 copy-done.23
  131.8 1.6 copy-done.25
  133.4 1.6 copy-done.27
  135.0 1.6 copy-done.29
  136.6 18.7 %scatter.4 = (f32[4104,128]{1,0:T(8,128)S(1)}, f32[4104,128]{1,0:T(8,128)}, f32[4104,128]{1,0:T(8,128)S(1)}, f32[4104,128]{1,0:T(8,128)S(1)}) custom-call(s32[1]{0:T(128)} %bitcast.s_ref, s32[8192]{0:T(1024)S(1)} %bitcast.14, s32[8192]{0:T(1024)S(1)} %bitcast.16, s32[8192]{0:T(1024)S(1)} %bitcast.18, f32[3072,128]{1,0:T(8,128)S(1)} %collective-permute-done.6.refs_3_, ...), custom_call_target="tpu_custom_call" | custom-call | flops 18432000000 | bytes 9437184 | tf_op jit(solution)/shard_map/scatter/pallas_call | solution.py:238
  155.3 3.1 %copy-done.20 = f32[4112,128]{1,0:T(8,128)S(1)} copy-done((f32[4112,128]{1,0:T(8,128)S(1)}, f32[4112,128]{1,0:T(8,128)}, u32[]{:S(2)}) %copy-start.20) | copy-done | bytes 2105368
  158.6 1.6 collective-permute-start.20
  160.3 1.4 collective-permute-start.17
  161.7 23.1 %collective-permute-done.20.refs_2_ = f32[2056,128]{1,0:T(8,128)S(1)} collective-permute-done((f32[2056,128]{1,0:T(8,128)S(1)}, f32[2056,128]{1,0:T(8,128)S(1)}, u32[]{:S(2)}, u32[]{:S(2)}) %collective-permute-start.20) | collective-permute-done | bytes 1052704 | tf_op jit(solution)/shard_map/ppermute | solution.py:338
  185.1 32.3 %collective-permute-start.21 = (f32[2056,128]{1,0:T(8,128)S(1)}, f32[2056,128]{1,0:T(8,128)}, u32[]{:S(2)}, u32[]{:S(2)}) collective-permute-start(f32[2056,128]{1,0:T(8,128)S(1)} %merge.12.refs_0_), channel_id=1, source_target_pairs={{0,4},{12,8},{1,5},{13,9},{2,6},{14,10},{3,7},{15,11},{16,20},{28,... | collective-permute-start | bytes 3158024 | tf_op jit(solution)/shard_map/ppermute | solution.py:382
  217.4 1.2 merge.9.refs_0_
  218.7 21.6 %collective-permute-start.18 = (f32[2056,128]{1,0:T(8,128)}, f32[2056,128]{1,0:T(8,128)}, u32[]{:S(2)}, u32[]{:S(2)}) collective-permute-start(f32[2056,128]{1,0:T(8,128)} %merge.9.refs_0_), channel_id=1, source_target_pairs={{0,4},{12,8},{1,5},{13,9},{2,6},{14,10},{3,7},{15,11},{16,20},{28,... | collective-permute-start | bytes 3158024 | tf_op jit(solution)/shard_map/ppermute | solution.py:382
  240.3 1.6 copy-done.18
  241.9 3.3 %merge.7 = f32[4104,128]{1,0:T(8,128)} custom-call(f32[4104,128]{1,0:T(8,128)S(1)} %copy-done.18, f32[4104,128]{1,0:T(8,128)} %collective-permute-done.13.refs_1_), custom_call_target="tpu_custom_call" | custom-call | flops 4000000000 | bytes 8388608 | tf_op jit(solution)/shard_map/merge/pallas_call | solution.py:270
  245.2 1.7 collective-permute-start.14
  246.9 2.3 merge.13
  249.2 1.3 collective-permute-start.22
  250.5 11.5 %collective-permute-done.18.refs_1_ = f32[2056,128]{1,0:T(8,128)} collective-permute-done((f32[2056,128]{1,0:T(8,128)}, f32[2056,128]{1,0:T(8,128)}, u32[]{:S(2)}, u32[]{:S(2)}) %collective-permute-start.18) | collective-permute-done | bytes 1052704 | tf_op jit(solution)/shard_map/ppermute | solution.py:382
  262.0 2.8 merge.10
  264.8 1.3 collective-permute-start.19
  266.1 27.4 %fusion.3 = (f32[64]{0:T(128)S(1)}, f32[64,8000]{1,0:T(8,128)S(1)}) fusion(bf16[4096,8000]{0,1:T(8,128)(2,1)} %param.7, bf16[256,4096]{1,0:T(8,128)(2,1)} %q_ref.3, s32[]{:T(128)S(6)} %select_n.3), kind=kOutput, calls=%fused_computation.5 | convolution fusion | flops 4194816000 | bytes 68108544 | tf_op jit(solution)/shard_map/dot_general | solution.py:390
  294.2 1.2 collective-permute-done.s1_ref
  295.4 1.5 collective-permute-start.1
  296.9 2.5 collective-permute-done.1.s2_ref
  300.5 2.5 collective-permute-done.2.s3_ref
  303.0 1.6 copy-done.16
  304.6 5.0 %final.1 = f32[64,8000]{1,0:T(8,128)} custom-call(s32[1]{0:T(128)} %bitcast.s_ref, f32[1]{0:T(128)} %bitcast.12.mix_ref, f32[64,8000]{1,0:T(8,128)S(1)} %get-tuple-element.54.logits_ref, f32[64,128]{1,0:T(8,128)S(1)} %pad_maximum_fusion.s0_ref, f32[64,128]{1,0:T(8,128)S(1)} %collective-permute-done.s1_ref, f32[64,128]{1,0:T(8,128)S(1)} %collective-permute-done.1.s2_ref, ...), custom_call_target="tpu_custom_call" | custom-call | flops 5000000000 | bytes 12582912 | tf_op jit(solution)/shard_map/final/pallas_call | solution.py:315
  (83 shorter events, 9.7 us)
Async XLA Ops:
  0.0 49.4 %collective-permute-start.3 = (s32[64,128]{1,0:T(8,128)}, s32[64,128]{1,0:T(8,128)S(1)}, u32[]{:S(2)}, u32[]{:S(2)}) collective-permute-start(s32[64,128]{1,0:T(8,128)} %bitcast.21), channel_id=1, source_target_pairs={{0,4},{4,0},{8,12},{12,8},{1,5},{5,1},{9,13},{13,9},{2,6},{6,2},{1... | collective-permute-start | bytes 98312 | tf_op jit(solution)/shard_map/ppermute | solution.py:351
  3.1 50.5 %collective-permute-start.4 = (s32[64,128]{1,0:T(8,128)}, s32[64,128]{1,0:T(8,128)S(1)}, u32[]{:S(2)}, u32[]{:S(2)}) collective-permute-start(s32[64,128]{1,0:T(8,128)} %bitcast.22), channel_id=1, source_target_pairs={{0,8},{12,4},{1,9},{13,5},{2,10},{14,6},{3,11},{15,7},{16,24},{28,... | collective-permute-start | bytes 98312 | tf_op jit(solution)/shard_map/ppermute | solution.py:351
  7.5 47.9 %collective-permute-start.5 = (s32[64,128]{1,0:T(8,128)}, s32[64,128]{1,0:T(8,128)S(1)}, u32[]{:S(2)}, u32[]{:S(2)}) collective-permute-start(s32[64,128]{1,0:T(8,128)} %bitcast.23), channel_id=1, source_target_pairs={{4,8},{8,4},{5,9},{9,5},{6,10},{10,6},{7,11},{11,7},{20,24},{24,20... | collective-permute-start | bytes 98312 | tf_op jit(solution)/shard_map/ppermute | solution.py:351
  8.9 1.6 copy-start
  21.9 37.4 %collective-permute-start.10 = (f32[1024,128]{1,0:T(8,128)}, f32[1024,128]{1,0:T(8,128)}, u32[]{:S(2)}, u32[]{:S(2)}) collective-permute-start(f32[1024,128]{1,0:T(8,128)} %get-tuple-element.38), channel_id=1, source_target_pairs={{0,8},{12,4},{1,9},{13,5},{2,10},{14,6},{3,11},{15,7},{16,24},{28,... | collective-permute-start | bytes 1572872 | tf_op jit(solution)/shard_map/ppermute | solution.py:353
  25.3 59.5 %collective-permute-start.11 = (f32[1024,128]{1,0:T(8,128)}, f32[1024,128]{1,0:T(8,128)}, u32[]{:S(2)}, u32[]{:S(2)}) collective-permute-start(f32[1024,128]{1,0:T(8,128)} %get-tuple-element.38), channel_id=1, source_target_pairs={{4,8},{8,4},{5,9},{9,5},{6,10},{10,6},{7,11},{11,7},{20,24},{24,20... | collective-permute-start | bytes 1572872 | tf_op jit(solution)/shard_map/ppermute | solution.py:354
  49.4 6.0 %copy-start.30 = (s32[64,128]{1,0:T(8,128)}, s32[64,128]{1,0:T(8,128)S(1)}, u32[]{:S(2)}) copy-start(s32[64,128]{1,0:T(8,128)S(1)} %collective-permute-done.3.refs_1_) | copy-start | bytes 98308
  49.4 79.4 %collective-permute-start.7 = (f32[3072,128]{1,0:T(8,128)S(1)}, f32[3072,128]{1,0:T(8,128)}, u32[]{:S(2)}, u32[]{:S(2)}) collective-permute-start(f32[3072,128]{1,0:T(8,128)S(1)} %get-tuple-element.33), channel_id=1, source_target_pairs={{0,8},{12,4},{1,9},{13,5},{2,10},{14,6},{3,11},{15,7},{16,24},{28,... | collective-permute-start | bytes 4718600 | tf_op jit(solution)/shard_map/ppermute | solution.py:357
  53.6 1.8 copy-start.31
  53.6 75.2 %collective-permute-start.8 = (f32[3072,128]{1,0:T(8,128)S(1)}, f32[3072,128]{1,0:T(8,128)}, u32[]{:S(2)}, u32[]{:S(2)}) collective-permute-start(f32[3072,128]{1,0:T(8,128)S(1)} %get-tuple-element.33), channel_id=1, source_target_pairs={{4,8},{8,4},{5,9},{9,5},{6,10},{10,6},{7,11},{11,7},{20,24},{24,20... | collective-permute-start | bytes 4718600 | tf_op jit(solution)/shard_map/ppermute | solution.py:358
  55.4 43.1 %collective-permute-start.9 = (f32[1024,128]{1,0:T(8,128)}, f32[1024,128]{1,0:T(8,128)}, u32[]{:S(2)}, u32[]{:S(2)}) collective-permute-start(f32[1024,128]{1,0:T(8,128)} %copy-done.7), channel_id=1, source_target_pairs={{0,4},{4,0},{8,12},{12,8},{1,5},{5,1},{9,13},{13,9},{2,6},{6,2},{1... | collective-permute-start | bytes 1572872 | tf_op jit(solution)/shard_map/ppermute | solution.py:355
  59.3 70.8 %collective-permute-start.6 = (f32[3072,128]{1,0:T(8,128)S(1)}, f32[3072,128]{1,0:T(8,128)S(1)}, u32[]{:S(2)}, u32[]{:S(2)}) collective-permute-start(f32[3072,128]{1,0:T(8,128)S(1)} %get-tuple-element.32), channel_id=1, source_target_pairs={{0,4},{4,0},{8,12},{12,8},{1,5},{5,1},{9,13},{13,9},{2,6},{6,2},{1... | collective-permute-start | bytes 4718600 | tf_op jit(solution)/shard_map/ppermute | solution.py:359
  60.8 1.4 copy-start.4
  64.0 34.6 %copy-start.2 = (f32[3072,128]{1,0:T(8,128)S(1)}, f32[3072,128]{1,0:T(8,128)}, u32[]{:S(2)}) copy-start(f32[3072,128]{1,0:T(8,128)} %copy-done.1) | copy-start | bytes 4718596
  64.0 34.6 %copy-start.6 = (f32[1024,128]{1,0:T(8,128)S(1)}, f32[1024,128]{1,0:T(8,128)}, u32[]{:S(2)}) copy-start(f32[1024,128]{1,0:T(8,128)} %copy-done.5) | copy-start | bytes 1572868
  64.0 34.6 %copy-start.10 = (s32[64,128]{1,0:T(8,128)S(1)}, s32[64,128]{1,0:T(8,128)}, u32[]{:S(2)}) copy-start(s32[64,128]{1,0:T(8,128)} %get-tuple-element.29) | copy-start | bytes 98308
  64.0 34.6 %copy-start.11 = (s32[64,128]{1,0:T(8,128)S(1)}, s32[64,128]{1,0:T(8,128)}, u32[]{:S(2)}) copy-start(s32[64,128]{1,0:T(8,128)} %get-tuple-element.30) | copy-start | bytes 98308
  64.0 34.6 %copy-start.12 = (s32[64,128]{1,0:T(8,128)S(1)}, s32[64,128]{1,0:T(8,128)}, u32[]{:S(2)}) copy-start(s32[64,128]{1,0:T(8,128)} %get-tuple-element.31) | copy-start | bytes 98308
  64.0 34.6 %copy-start.14 = (s32[64,128]{1,0:T(8,128)S(1)}, s32[64,128]{1,0:T(8,128)}, u32[]{:S(2)}) copy-start(s32[64,128]{1,0:T(8,128)} %get-tuple-element.34) | copy-start | bytes 98308
  83.4 1.3 copy-start.19
  84.8 70.5 %collective-permute-start.16 = (f32[4112,128]{1,0:T(8,128)S(1)}, f32[4112,128]{1,0:T(8,128)S(1)}, u32[]{:S(2)}, u32[]{:S(2)}) collective-permute-start(f32[4112,128]{1,0:T(8,128)S(1)} %get-tuple-element.52), channel_id=1, source_target_pairs={{0,1},{1,0},{2,3},{3,2},{4,5},{5,4},{6,7},{7,6},{8,9},{9,8},{10,11... | collective-permute-start | bytes 6316040 | tf_op jit(solution)/shard_map/ppermute | solution.py:338
  98.6 63.2 %collective-permute-start.15 = (f32[4112,128]{1,0:T(8,128)S(1)}, f32[4112,128]{1,0:T(8,128)S(1)}, u32[]{:S(2)}, u32[]{:S(2)}) collective-permute-start(f32[4112,128]{1,0:T(8,128)S(1)} %get-tuple-element.50), channel_id=1, source_target_pairs={{0,1},{1,0},{2,3},{3,2},{4,5},{5,4},{6,7},{7,6},{8,9},{9,8},{10,11... | collective-permute-start | bytes 6316040 | tf_op jit(solution)/shard_map/ppermute | solution.py:338
  123.4 1.4 copy-start.22
  124.8 1.3 copy-start.24
  126.2 1.4 copy-start.26
  127.5 1.3 copy-start.28
  130.2 1.6 copy-start.23
  131.8 1.6 copy-start.25
  133.4 1.6 copy-start.27
  135.0 1.6 copy-start.29
  155.2 3.3 %copy-start.15 = (f32[4104,128]{1,0:T(8,128)}, f32[4104,128]{1,0:T(8,128)S(1)}, u32[]{:S(2)}) copy-start(f32[4104,128]{1,0:T(8,128)S(1)} %get-tuple-element.43.keep_ref) | copy-start | bytes 6303748
  155.2 3.3 %copy-start.17 = (f32[4104,128]{1,0:T(8,128)}, f32[4104,128]{1,0:T(8,128)S(1)}, u32[]{:S(2)}) copy-start(f32[4104,128]{1,0:T(8,128)S(1)} %get-tuple-element.45.refs_0_) | copy-start | bytes 6303748
  155.3 3.1 %copy-start.20 = (f32[4112,128]{1,0:T(8,128)S(1)}, f32[4112,128]{1,0:T(8,128)}, u32[]{:S(2)}) copy-start(f32[4112,128]{1,0:T(8,128)} %copy-done.19) | copy-start | bytes 6316036
  158.4 1.8 copy-start.21
  158.6 26.2 %collective-permute-start.20 = (f32[2056,128]{1,0:T(8,128)S(1)}, f32[2056,128]{1,0:T(8,128)S(1)}, u32[]{:S(2)}, u32[]{:S(2)}) collective-permute-start(f32[2056,128]{1,0:T(8,128)S(1)} %merge.11), channel_id=1, source_target_pairs={{0,2},{1,3},{2,0},{3,1},{4,6},{5,7},{6,4},{7,5},{8,10},{9,11},{10,... | collective-permute-start | bytes 3158024 | tf_op jit(solution)/shard_map/ppermute | solution.py:338
  160.2 80.2 %collective-permute-start.13 = (f32[4104,128]{1,0:T(8,128)S(1)}, f32[4104,128]{1,0:T(8,128)}, u32[]{:S(2)}, u32[]{:S(2)}) collective-permute-start(f32[4104,128]{1,0:T(8,128)S(1)} %get-tuple-element.46), channel_id=1, source_target_pairs={{0,1},{1,0},{2,3},{3,2},{4,5},{5,4},{6,7},{7,6},{8,9},{9,8},{10,11... | collective-permute-start | bytes 6303752 | tf_op jit(solution)/shard_map/ppermute | solution.py:338
  160.3 57.1 %collective-permute-start.17 = (f32[2056,128]{1,0:T(8,128)S(1)}, f32[2056,128]{1,0:T(8,128)S(1)}, u32[]{:S(2)}, u32[]{:S(2)}) collective-permute-start(f32[2056,128]{1,0:T(8,128)S(1)} %merge.8), channel_id=1, source_target_pairs={{0,2},{1,3},{2,0},{3,1},{4,6},{5,7},{6,4},{7,5},{8,10},{9,11},{10,... | collective-permute-start | bytes 3158024 | tf_op jit(solution)/shard_map/ppermute | solution.py:338
  185.1 61.8 %collective-permute-start.21 = (f32[2056,128]{1,0:T(8,128)S(1)}, f32[2056,128]{1,0:T(8,128)}, u32[]{:S(2)}, u32[]{:S(2)}) collective-permute-start(f32[2056,128]{1,0:T(8,128)S(1)} %merge.12.refs_0_), channel_id=1, source_target_pairs={{0,4},{12,8},{1,5},{13,9},{2,6},{14,10},{3,7},{15,11},{16,20},{28,... | collective-permute-start | bytes 3158024 | tf_op jit(solution)/shard_map/ppermute | solution.py:382
  218.7 43.4 %collective-permute-start.18 = (f32[2056,128]{1,0:T(8,128)}, f32[2056,128]{1,0:T(8,128)}, u32[]{:S(2)}, u32[]{:S(2)}) collective-permute-start(f32[2056,128]{1,0:T(8,128)} %merge.9.refs_0_), channel_id=1, source_target_pairs={{0,4},{12,8},{1,5},{13,9},{2,6},{14,10},{3,7},{15,11},{16,20},{28,... | collective-permute-start | bytes 3158024 | tf_op jit(solution)/shard_map/ppermute | solution.py:382
  240.3 62.7 %collective-permute-start.12 = (f32[4104,128]{1,0:T(8,128)}, f32[4104,128]{1,0:T(8,128)}, u32[]{:S(2)}, u32[]{:S(2)}) collective-permute-start(f32[4104,128]{1,0:T(8,128)} %get-tuple-element.44), channel_id=1, source_target_pairs={{0,1},{1,0},{2,3},{3,2},{4,5},{5,4},{6,7},{7,6},{8,9},{9,8},{10,11... | collective-permute-start | bytes 6303752 | tf_op jit(solution)/shard_map/ppermute | solution.py:338
  240.3 1.6 copy-start.18
  245.2 57.9 %collective-permute-start.14 = (f32[4104,128]{1,0:T(8,128)}, f32[4104,128]{1,0:T(8,128)}, u32[]{:S(2)}, u32[]{:S(2)}) collective-permute-start(f32[4104,128]{1,0:T(8,128)} %merge.7), channel_id=1, source_target_pairs={{0,2},{1,3},{2,0},{3,1},{4,6},{5,7},{6,4},{7,5},{8,10},{9,11},{10,... | collective-permute-start | bytes 6303752 | tf_op jit(solution)/shard_map/ppermute | solution.py:338
  249.2 53.8 %collective-permute-start.22 = (f32[2056,128]{1,0:T(8,128)}, f32[2056,128]{1,0:T(8,128)S(1)}, u32[]{:S(2)}, u32[]{:S(2)}) collective-permute-start(f32[2056,128]{1,0:T(8,128)} %merge.13), channel_id=1, source_target_pairs={{4,12},{8,0},{5,13},{9,1},{6,14},{10,2},{7,15},{11,3},{20,28},{24,... | collective-permute-start | bytes 3158024 | tf_op jit(solution)/shard_map/ppermute | solution.py:384
  264.8 38.2 %collective-permute-start.19 = (f32[2056,128]{1,0:T(8,128)}, f32[2056,128]{1,0:T(8,128)}, u32[]{:S(2)}, u32[]{:S(2)}) collective-permute-start(f32[2056,128]{1,0:T(8,128)} %merge.10), channel_id=1, source_target_pairs={{4,12},{8,0},{5,13},{9,1},{6,14},{10,2},{7,15},{11,3},{20,28},{24,... | collective-permute-start | bytes 3158024 | tf_op jit(solution)/shard_map/ppermute | solution.py:384
  294.2 1.2 collective-permute-start
  295.4 3.9 %collective-permute-start.1 = (f32[64,128]{1,0:T(8,128)S(1)}, f32[64,128]{1,0:T(8,128)S(1)}, u32[]{:S(2)}, u32[]{:S(2)}) collective-permute-start(f32[64,128]{1,0:T(8,128)S(1)} %pad_maximum_fusion.s0_ref), channel_id=1, source_target_pairs={{0,2},{1,3},{2,0},{3,1},{4,6},{5,7},{6,4},{7,5},{8,10},{9,11},{10,... | collective-permute-start | bytes 98312 | tf_op jit(solution)/shard_map/ppermute | solution.py:338
  299.3 3.7 %collective-permute-start.2 = (f32[64,128]{1,0:T(8,128)S(1)}, f32[64,128]{1,0:T(8,128)S(1)}, u32[]{:S(2)}, u32[]{:S(2)}) collective-permute-start(f32[64,128]{1,0:T(8,128)S(1)} %pad_maximum_fusion.s0_ref), channel_id=1, source_target_pairs={{0,3},{1,2},{2,1},{3,0},{4,7},{5,6},{6,5},{7,4},{8,11},{9,10},{10,... | collective-permute-start | bytes 98312 | tf_op jit(solution)/shard_map/ppermute | solution.py:338
  303.0 1.6 copy-start.16
  (8 other events, 7.1 us)

commit v2 on v1

v2 whole, which is shorter than its diff:
```python
import functools

import jax
import jax.numpy as jnp
from jax import lax
from jax.experimental import pallas as pl
from jax.experimental.pallas import tpu as pltpu
from jax.sharding import PartitionSpec as P


LANES = 128
BLOCK = 512
BATCH = 16
WIDE = 2
VOCAB_LOC = 8000
PIECE = 4096
FIRST = 6
META = 8
SLOTS = 4
OUT_GROUP = 2
TOK_ROWS = 64
MERGE_STEPS = 4
VMEM = 66_900_000
STEP = 976
UPPER = VOCAB_LOC - PIECE
FLAG = 1 << 16
CLASH = 1 << 17


def targets(me):
    left = me < 2
    return me, me ^ 1, jnp.where(left, 2, 1), jnp.where(left, 3, 0)


def codes_of(tok, me):
    owner = sum((tok >= VOCAB_LOC * i).astype(jnp.int32) for i in (1, 2, 3))
    code = tok - owner * VOCAB_LOC + (owner ^ me) * VOCAB_LOC
    lane = lax.broadcasted_iota(jnp.int32, code.shape, 1)
    place = lane % BATCH
    clash = jnp.zeros_like(code)
    for d in range(1, BATCH):
        same = (code == pltpu.roll(code, LANES - d, 1)) & (place < BATCH - d)
        clash = clash | same.astype(jnp.int32)
    d = BATCH // 2
    while d:
        clash = clash | pltpu.roll(clash, LANES - d, 1)
        d //= 2
    first = place == 0
    group = jnp.max(jnp.where(first, clash, 0), axis=1, keepdims=True)
    marks = FLAG + jnp.where(clash > 0, CLASH, 0)
    return code + jnp.where(first & (group > 0), marks, 0)


def scores_kernel(first, count, carried, s_ref, m_ref, tau_ref, q_hbm, k_hbm, tok_ref, *refs):
    refs = refs[2:] if carried else refs
    outs, refs = refs[:4], refs[4:]
    if not carried:
        code_hbm, refs = refs[0], refs[1:]
    q_ref, qs_ref, held, stage, code_i, code_f, sem, q_sem, out_sem, tok_sem = refs
    half = BLOCK // 2
    group = OUT_GROUP * half

    def fetch(block):
        slot = lax.rem(block, SLOTS)
        rows = pl.ds(pl.multiple_of((first + block) * BLOCK, BLOCK), BLOCK)
        return pltpu.make_async_copy(k_hbm.at[rows], held.at[slot], sem.at[slot])

    def save(g):
        copies = []
        for i, out in enumerate(outs):
            start = g * group + (0 if i in (1, 2) else first * half)
            rows = pl.ds(pl.multiple_of(start, half), group)
            copies.append(pltpu.make_async_copy(stage.at[i, pl.ds(pl.multiple_of(g * group, half), group)], out.at[rows], out_sem.at[i, g]))
        return copies

    load_q = pltpu.make_async_copy(q_hbm, q_ref, q_sem)
    load_q.start()
    fetch(0).start()
    tokens = []
    if not carried:
        code_i[...] = codes_of(tok_ref[...], m_ref[0])
        code_f[...] = code_i[...].astype(jnp.float32)
        at = {1: outs[1].shape[0] - TOK_ROWS, 2: outs[2].shape[0] - TOK_ROWS}
        tokens = [pltpu.make_async_copy(code_f, outs[i].at[pl.ds(at[i], TOK_ROWS)], tok_sem.at[i - 1]) for i in (1, 2)]
        tokens.append(pltpu.make_async_copy(code_i, code_hbm, tok_sem.at[2]))
        for copy in tokens:
            copy.start()
    load_q.wait()
    for block in range(1, SLOTS - 1):
        fetch(block).start()
    for k, z in enumerate(targets(s_ref[0])):
        qs_ref[64 * k:64 * k + 64, :] = q_ref[pl.ds(pl.multiple_of(z * 64, 64), 64), :]
    low = lax.broadcasted_iota(jnp.int32, (half, LANES), 1) < 64

    @pl.loop(0, count)
    def _(block):
        @pl.when(block + SLOTS - 1 < count)
        def _():
            fetch(block + SLOTS - 1).start()

        fetch(block).wait()
        keys = held[lax.rem(block, SLOTS)]
        dots = lax.dot_general(keys, qs_ref[...], (((1,), (1,)), ((), ())), preferred_element_type=jnp.float32)
        wide = keys.astype(jnp.float32)
        norms = jnp.sum(wide * wide, axis=1, keepdims=True)
        scores = (2.0 * dots - norms) / tau_ref[0]
        out = pl.ds(pl.multiple_of(block * half, half), half)
        for k in range(4):
            tile = scores[:, LANES * (k // 2):LANES * (k // 2) + LANES]
            top, bottom = tile[:half], tile[half:]
            if k % 2 == 0:
                stage[k, out, :] = jnp.where(low, top, pltpu.roll(bottom, 64, 1))
            else:
                stage[k, out, :] = jnp.where(low, pltpu.roll(top, 64, 1), bottom)

        @pl.when(lax.rem(block, OUT_GROUP) == OUT_GROUP - 1)
        def _():
            for copy in save(block // OUT_GROUP):
                copy.start()

    for g in range(count // OUT_GROUP):
        for copy in save(g):
            copy.wait()
    for copy in tokens:
        copy.wait()


def score_call(me, model, tau, queries, keys, tok2, first, count, prev):
    width = keys.shape[1]
    whole = keys.shape[0] // 2
    rows = count * BLOCK // 2
    smem = pl.BlockSpec(memory_space=pltpu.SMEM)
    hbm = pl.BlockSpec(memory_space=pltpu.HBM)
    sent = (rows + (0 if prev else TOK_ROWS), LANES)
    shapes = [(whole, LANES), sent, sent, (whole, LANES)]
    return pl.pallas_call(
        functools.partial(scores_kernel, first, count, bool(prev)),
        in_specs=[smem, smem, smem, hbm, hbm, pl.BlockSpec(memory_space=pltpu.VMEM)] + [hbm] * len(prev),
        out_specs=[hbm] * (4 if prev else 5),
        out_shape=[jax.ShapeDtypeStruct(shape, jnp.float32) for shape in shapes] + ([] if prev else [jax.ShapeDtypeStruct(tok2.shape, jnp.int32)]),
        scratch_shapes=[
            pltpu.VMEM(queries.shape, queries.dtype),
            pltpu.VMEM(queries.shape, queries.dtype),
            pltpu.VMEM((SLOTS, BLOCK, width), keys.dtype),
            pltpu.VMEM((4, rows, LANES), jnp.float32),
            pltpu.VMEM((TOK_ROWS, LANES), jnp.int32),
            pltpu.VMEM((TOK_ROWS, LANES), jnp.float32),
            pltpu.SemaphoreType.DMA((SLOTS,)),
            pltpu.SemaphoreType.DMA,
            pltpu.SemaphoreType.DMA((4, count // OUT_GROUP)),
            pltpu.SemaphoreType.DMA((3,)),
        ],
        input_output_aliases={6: 0, 7: 3} if prev else {},
        compiler_params=pltpu.CompilerParams(vmem_limit_bytes=VMEM),
        cost_estimate=pl.CostEstimate(flops=2 * count * BLOCK * width * 256, bytes_accessed=count * BLOCK * width * 2, transcendentals=0),
        name="scores",
    )(me, model, tau, queries, keys, tok2, *prev)


def fold(row, op):
    wide = jnp.broadcast_to(row, (8, LANES))
    return op(wide, pltpu.roll(wide, 64, 1))[:1]


def scatter_kernel(segments, n_codes, chunks, carried, s_ref, *refs):
    n_x = len(segments)
    code_hbms, refs = refs[:n_codes], refs[n_codes:]
    x_hbms, refs = refs[:n_x], refs[n_x:]
    if carried:
        prev_hbms, refs = refs[:4], refs[4:]
    piece_hbms, refs = refs[:4], refs[4:]
    hist, e_ref, z_ref, stage, sem, prev_sem, out_sem = refs[:7]
    x_refs, refs = refs[7:7 + n_x], refs[7 + n_x:]
    code_refs, refs = refs[:n_codes], refs[n_codes:]
    piece_refs = [stage.at[rel] for rel in range(4)]
    half = BLOCK // 2
    loads = [pltpu.make_async_copy(a.at[pl.ds(0, b.shape[0])], b, sem.at[i]) for i, (a, b) in enumerate(zip(x_hbms, x_refs))]
    loads += [pltpu.make_async_copy(a, b, sem.at[n_x + i]) for i, (a, b) in enumerate(zip(code_hbms, code_refs))]
    for load in loads:
        load.start()
    if carried:
        prev, = refs
        prev_refs = [prev.at[rel] for rel in range(4)]
        prev_loads = [pltpu.make_async_copy(a, prev.at[i], prev_sem.at[i]) for i, a in enumerate(prev_hbms)]
        for load in prev_loads:
            load.start()
    saves = [pltpu.make_async_copy(stage.at[rel], piece_hbms[rel], out_sem.at[rel]) for rel in range(4)]

    @pl.loop(0, hist.shape[0] // 320)
    def _(i):
        hist[pl.ds(pl.multiple_of(i * 320, 320), 320), :] = jnp.zeros((320, LANES), jnp.float32)

    z_ref[...] = jnp.zeros_like(z_ref)
    for load in loads:
        load.wait()
    middle = (s_ref[0] == 1) | (s_ref[0] == 2)
    counts = [jnp.where(middle, x.shape[0] // (WIDE * half), 0) if seg[2] else x.shape[0] // (WIDE * half) for x, seg in zip(x_refs, segments)]
    peak = jnp.full((8, LANES), -jnp.inf, jnp.float32)
    for x_ref, count in zip(x_refs, counts):
        def widen(block, peak):
            x = x_ref[pl.ds(pl.multiple_of(block * WIDE * half, WIDE * half), WIDE * half), :]
            return jnp.maximum(peak, jnp.max(x.reshape(WIDE * half // 8, 8, LANES), axis=0))

        peak = lax.fori_loop(0, count, widen, peak)
    top = fold(jnp.max(peak, axis=0, keepdims=True), jnp.maximum)

    for x_ref, (which, base, _), count in zip(x_refs, segments, counts):
        code_ref = code_refs[which]

        @pl.loop(0, count)
        def _(block):
            wide = pl.ds(pl.multiple_of(block * WIDE * half, WIDE * half), WIDE * half)
            e = jnp.exp(x_ref[wide, :] - top)
            z_ref[...] += jnp.sum(e.reshape(WIDE * half // 8, 8, LANES), axis=0)
            for i in range(WIDE):
                part = e[i * half:i * half + half]
                e_ref[i * BLOCK:i * BLOCK + half] = part
                e_ref[i * BLOCK + half:i * BLOCK + BLOCK] = pltpu.roll(part, 64, 1)

            @pl.loop(0, WIDE * BLOCK // LANES)
            def _(group):
                row = pl.multiple_of(group * LANES, LANES)
                at = pl.multiple_of(base + block * WIDE * BLOCK + group * LANES, LANES)
                rows_ref = e_ref.at[pl.ds(row, LANES)]
                head = code_ref[at]

                @pl.when(head < FLAG)
                def _():
                    for b in range(0, LANES, BATCH):
                        ids = [code_ref.at[pl.ds(b + i, code_ref.shape[0] - LANES + 1)][at] for i in range(BATCH)]
                        new = [hist[pl.ds(ids[i], 1), :] + rows_ref[b + i:b + i + 1, :] for i in range(BATCH)]
                        for i in range(BATCH):
                            hist[pl.ds(ids[i], 1), :] = new[i]

                @pl.when(head >= FLAG)
                def _():
                    @pl.loop(0, LANES // BATCH)
                    def _(b):
                        mark = code_ref[at + b * BATCH]
                        ids = [mark & (FLAG - 1)] + [code_ref[at + b * BATCH + i] for i in range(1, BATCH)]
                        rows = rows_ref.at[pl.ds(pl.multiple_of(b * BATCH, BATCH), BATCH)]

                        @pl.when((mark & CLASH) == 0)
                        def _():
                            new = [hist[pl.ds(ids[i], 1), :] + rows[i:i + 1, :] for i in range(BATCH)]
                            for i in range(BATCH):
                                hist[pl.ds(ids[i], 1), :] = new[i]

                        @pl.when((mark & CLASH) != 0)
                        def _():
                            for i in range(BATCH):
                                hist[pl.ds(ids[i], 1), :] += rows[i:i + 1, :]

    size = PIECE // chunks
    z = fold(jnp.sum(z_ref[...], axis=0, keepdims=True), jnp.add)
    scale = held_scale = None
    if carried:
        for load in prev_loads:
            load.wait()
        held_top = prev_refs[0][size + 1:size + 2, :]
        both = jnp.maximum(top, held_top)
        scale, held_scale = jnp.exp(top - both), jnp.exp(held_top - both)
        z = z * scale + prev_refs[0][size:size + 1, :] * held_scale
        top = both
    meta = jnp.concatenate([z, top, jnp.zeros((META - 2, LANES), jnp.float32)], axis=0)

    def place(rel, c, at, rows, both):
        first = c * size + at
        lower = hist[pl.ds(pl.multiple_of(rel * VOCAB_LOC + first, 8), rows), :]
        low = lax.broadcasted_iota(jnp.int32, (rows, LANES), 1) < 64
        if both:
            value = jnp.where(low, lower, pltpu.roll(hist[pl.ds(pl.multiple_of(rel * VOCAB_LOC + PIECE + first, 8), rows), :], 64, 1))
        else:
            value = jnp.where(low, lower, 0.0)
        if carried:
            value = value * scale + prev_refs[rel][pl.ds(pl.multiple_of(first + c * META, 8), rows), :] * held_scale
        piece_refs[rel][pl.ds(pl.multiple_of(c * (size + META) + at, 8), rows), :] = value

    for rel in (3, 1, 2, 0):
        for c in range(chunks):
            full = min(size, UPPER - c * size)

            @pl.loop(0, full // STEP)
            def _(i):
                place(rel, c, i * STEP, STEP, True)

            rest = full % STEP
            if rest:
                place(rel, c, full - rest, rest, True)
            if full < size:
                place(rel, c, full, size - full, False)
            at = c * (size + META) + size
            piece_refs[rel][at:at + META, :] = meta
        saves[rel].start()
    for save in saves:
        save.wait()


def scatter_call(s1, codes, xs, segments, prev):
    n_codes = len(codes)
    carried = prev is not None
    smem = pl.BlockSpec(memory_space=pltpu.SMEM)
    hbm = pl.BlockSpec(memory_space=pltpu.HBM)
    piece = jax.ShapeDtypeStruct((PIECE + CHUNKS * META, LANES), jnp.float32)
    n_keys = sum(2 * seg[0] for seg in segments)
    whole = pltpu.VMEM((4, *piece.shape), jnp.float32)
    return pl.pallas_call(
        functools.partial(scatter_kernel, tuple(seg[1:] for seg in segments), n_codes, CHUNKS, carried),
        in_specs=[smem] + [hbm] * (n_codes + len(xs) + (4 if carried else 0)),
        out_specs=[hbm] * 4,
        out_shape=[piece] * 4,
        scratch_shapes=[
            pltpu.VMEM((4 * VOCAB_LOC, LANES), jnp.float32),
            pltpu.VMEM((WIDE * BLOCK, LANES), jnp.float32),
            pltpu.VMEM((8, LANES), jnp.float32),
            whole,
            pltpu.SemaphoreType.DMA((len(xs) + n_codes,)),
            pltpu.SemaphoreType.DMA((4,)),
            pltpu.SemaphoreType.DMA((4,)),
        ]
        + [pltpu.VMEM((seg[0], LANES), jnp.float32) for seg in segments]
        + [pltpu.SMEM(c.shape, jnp.int32) for c in codes]
        + ([whole] if carried else []),
        compiler_params=pltpu.CompilerParams(vmem_limit_bytes=VMEM),
        cost_estimate=pl.CostEstimate(flops=n_keys * 1_000_000, bytes_accessed=n_keys * 512, transcendentals=n_keys * 64),
        name="scatter",
    )(s1, *codes, *xs, *(prev if carried else ()))


def merge_kernel(size, offsets, *refs):
    n = len(offsets)
    srcs, out_hbm, (stage, sem, out_sem, *bufs) = refs[:n], refs[n], refs[n + 1:]
    step = size // MERGE_STEPS
    parts = [(size, META)] + [(i * step, step) for i in range(MERGE_STEPS)]
    loads = [[pltpu.make_async_copy(r.at[pl.ds(o + at, rows)], b.at[pl.ds(at, rows)], sem.at[i, j]) for i, (r, o, b) in enumerate(zip(srcs, offsets, bufs))] for j, (at, rows) in enumerate(parts)]
    saves = [pltpu.make_async_copy(stage.at[pl.ds(at, rows)], out_hbm.at[pl.ds(at, rows)], out_sem.at[j]) for j, (at, rows) in enumerate(parts)]
    for group in loads:
        for load in group:
            load.start()
    for j, (at, rows) in enumerate(parts):
        for load in loads[j]:
            load.wait()
        if j == 0:
            tops = [b[size + 1:size + 2, :] for b in bufs]
            top = functools.reduce(jnp.maximum, tops)
            scales = [jnp.exp(t - top) for t in tops]
        total = functools.reduce(jnp.add, [b[at:at + rows, :] * f for b, f in zip(bufs, scales)])
        if j == 0:
            total = jnp.where(lax.broadcasted_iota(jnp.int32, (META, LANES), 0) == 1, top, total)
        stage[at:at + rows, :] = total
        saves[j].start()
    for save in saves:
        save.wait()


def merge_call(size, parts):
    hbm = pl.BlockSpec(memory_space=pltpu.HBM)
    shape = (size + META, LANES)
    return pl.pallas_call(
        functools.partial(merge_kernel, size, tuple(c * (size + META) for _, c in parts)),
        in_specs=[hbm] * len(parts),
        out_specs=hbm,
        out_shape=jax.ShapeDtypeStruct(shape, jnp.float32),
        scratch_shapes=[pltpu.VMEM(shape, jnp.float32), pltpu.SemaphoreType.DMA((len(parts), MERGE_STEPS + 1)), pltpu.SemaphoreType.DMA((MERGE_STEPS + 1,))] + [pltpu.VMEM(shape, jnp.float32)] * len(parts),
        compiler_params=pltpu.CompilerParams(vmem_limit_bytes=VMEM),
        cost_estimate=pl.CostEstimate(flops=4_000_000_000, bytes_accessed=size * 2048, transcendentals=0),
        name="merge",
    )(*[a for a, _ in parts])


def final_kernel(chunks, s_ref, mix_ref, logits_ref, s0_ref, s1_ref, s2_ref, s3_ref, keep_ref, mate_ref, *refs):
    y_refs, far_refs, out_ref = refs[:chunks], refs[chunks:2 * chunks], refs[2 * chunks]
    mix = mix_ref[0]
    end = (s_ref[0] == 0) | (s_ref[0] == 3)
    size = PIECE // chunks
    metas = [r[size:size + META, :] for r in (keep_ref, mate_ref, y_refs[0], far_refs[0])]
    tops = [t[1:2] for t in metas]
    tops[3] = jnp.where(end, tops[3], -jnp.inf)
    top = functools.reduce(jnp.maximum, tops)
    scales = [jnp.exp(t - top) for t in tops]
    z = sum(t[0:1] * f for t, f in zip(metas, scales))
    scales = [f * (mix / z) for f in scales]
    stats = [r[...] for r in (s0_ref, s1_ref, s2_ref, s3_ref)]
    lm_top = functools.reduce(jnp.maximum, [t[:, :1] for t in stats])
    total = sum(t[:, 64:65] * jnp.exp(t[:, :1] - lm_top) for t in stats)
    lm_scale = (1.0 - mix) / total

    def lm(at, count):
        return jnp.exp(logits_ref[:, at:at + count] - lm_top) * lm_scale

    for i in range(0, PIECE, LANES):
        c, at = i // size, i % size
        base = c * (size + META) + at
        parts = [keep_ref[base:base + LANES, :], mate_ref[base:base + LANES, :], y_refs[c][at:at + LANES, :], far_refs[c][at:at + LANES, :]]
        h = sum(p * f for p, f in zip(parts, scales))
        h = h.T
        out_ref[:, i:i + LANES] = jnp.log(h[:64] + lm(i, LANES))
        count = min(LANES, UPPER - i)
        if count > 0:
            out_ref[:, PIECE + i:PIECE + i + count] = jnp.log(h[64:, :count] + lm(PIECE + i, count))


def final_call(s1, mix, logits, stats, keep, mate, from_y, far):
    vmem = pl.BlockSpec(memory_space=pltpu.VMEM)
    smem = pl.BlockSpec(memory_space=pltpu.SMEM)
    return pl.pallas_call(
        functools.partial(final_kernel, len(far)),
        in_specs=[smem, smem] + [vmem] * (7 + 2 * len(far)),
        out_specs=vmem,
        out_shape=jax.ShapeDtypeStruct(logits.shape, jnp.float32),
        compiler_params=pltpu.CompilerParams(vmem_limit_bytes=40 * 1024 * 1024),
        cost_estimate=pl.CostEstimate(flops=5_000_000_000, bytes_accessed=12 << 20, transcendentals=1 << 20),
        name="final",
    )(s1, mix, logits, *stats, keep, mate, *from_y, *far)


NEAR = [(0, 1), (1, 0), (2, 3), (3, 2)]
FAR2 = [(0, 2), (3, 1)]
FAR1 = [(1, 2), (2, 1)]
INWARD = [(0, 1), (3, 2)]
ACROSS = [(1, 3), (2, 0)]
CHUNKS = 2


def solution(mesh):
    store_devs = mesh.shape["store"]

    def swap(x, axis, bit):
        return lax.ppermute(x, axis, [(i, i ^ bit) for i in range(4)])

    def local_step(queries, w_head, store_keys, store_tok, temperature, mix_weight):
        rows_loc = queries.shape[0] // store_devs
        s = lax.axis_index("store")
        m = lax.axis_index("model")
        s1, m1 = s.reshape(1), m.reshape(1)
        tau = temperature.reshape(1)
        blocks = store_keys.shape[0] // BLOCK
        n_a = FIRST * BLOCK
        size = PIECE // CHUNKS
        tok2 = store_tok.reshape(-1, LANES)

        toks = [lax.ppermute(tok2, "store", NEAR), lax.ppermute(tok2, "store", FAR2), lax.ppermute(tok2, "store", FAR1)]
        rows_a = n_a // 2
        rows_b = store_keys.shape[0] // 2 - rows_a
        own, near_a, sparse_a, dense, code_own = score_call(s1, m1, tau, queries, store_keys, tok2, 0, FIRST, [])
        far2_a = lax.ppermute(sparse_a, "store", FAR2)
        far1_a = lax.ppermute(sparse_a, "store", FAR1)
        near_a = lax.ppermute(near_a, "store", NEAR)
        own, near_b, sparse_b, dense = score_call(s1, m1, tau, queries, store_keys, tok2, FIRST, blocks - FIRST, [own, dense])
        far2_b = lax.ppermute(sparse_b, "store", FAR2)
        far1_b = lax.ppermute(sparse_b, "store", FAR1)
        near_b = lax.ppermute(near_b, "store", NEAR)
        code_own = code_own.reshape(-1)
        code_far2, code_far1, code_near = [x[-TOK_ROWS:].astype(jnp.int32).reshape(-1) for x in (far2_a, far1_a, near_a)]

        dense = scatter_call(s1, [code_own], [dense], ((rows_a + rows_b, 0, 0, False),), None)
        d_next = swap(dense[3], "model", 1)
        d_mate = swap(dense[1], "model", 1)
        d_y = []
        for c in range(CHUNKS):
            part = merge_call(size, [(dense[2], c), (d_next, c)])
            d_y.append(swap(part, "model", 2))

        segments = ((rows_a + rows_b, 0, 0, False), (rows_a, 1, 0, False), (rows_a, 2, 0, True), (rows_a, 3, 0, True))
        part = scatter_call(s1, [code_own, code_near, code_far2, code_far1], [own, near_a, far2_a, far1_a], segments, None)
        segments = ((rows_b, 0, n_a, False), (rows_b, 1, n_a, True), (rows_b, 2, n_a, True))
        keep, mate, ynext, matey = scatter_call(s1, [code_near, code_far2, code_far1], [near_b, far2_b, far1_b], segments, part)
        matey = swap(matey, "model", 1)
        mate = swap(mate, "model", 1)

        far = []
        for c in range(CHUNKS):
            plane = merge_call(size, [(dense[0], c), (d_mate, c), (d_y[c], 0)])
            inward = lax.ppermute(plane, "store", INWARD)
            pair = merge_call(size, [(plane, 0), (inward, 0)])
            far.append(lax.ppermute(pair, "store", ACROSS))

        from_y = []
        for c in range(CHUNKS):
            part = merge_call(size, [(ynext, c), (matey, c)])
            from_y.append(swap(part, "model", 2))

        my_rows = lax.dynamic_slice_in_dim(queries, s * rows_loc, rows_loc, axis=0)
        logits = lax.dot_general(my_rows, w_head, (((1,), (0,)), ((), ())), preferred_element_type=jnp.float32)
        lm_top = jnp.max(logits, axis=1, keepdims=True)
        lm_sum = jnp.sum(jnp.exp(logits - lm_top), axis=1, keepdims=True)
        stats = jnp.concatenate([jnp.broadcast_to(lm_top, (rows_loc, 64)), jnp.broadcast_to(lm_sum, (rows_loc, 64))], axis=1)
        stats = [stats] + [swap(stats, "model", k) for k in (1, 2, 3)]
        return final_call(s1, mix_weight.reshape(1), logits, stats, keep, mate, from_y, far)

    return jax.shard_map(local_step, mesh=mesh, in_specs=(P("data", None), P(None, "model"), P(("store", "model"), None), P(("store", "model")), P(), P()), out_specs=P(("data", "store"), "model"), check_vma=False)
```

time: 311 us -> 322 us (1.035)
  waiting for transfers between devices: 55.9 us -> 110 us
  starting transfers between devices: 83.6 us -> 55.3 us
  local copies, waits for them, and re-layouts: 29.6 us -> 4.62 us
  Pallas kernels: 111 us -> 118 us
  other arithmetic: 0.58 us -> 4.69 us
    unnamed x66 -> x6, local copies, waits for them, and re-layouts: 29.5 us -> 4.48 us
    ppermute x2, starting transfers between devices: 54 us -> 30.3 us  [local_step(): inward = lax.ppermute(plane, 'store', INWARD)]
    ppermute x2, waiting for transfers between devices: 11.5 us -> 32 us  [local_step(): inward = lax.ppermute(plane, 'store', INWARD)]
    ppermute x10 -> x11, waiting for transfers between devices: 29.3 us -> 49.6 us  [swap(): return lax.ppermute(x, axis, [(i, i ^ bit) for i in range(4)])]
    pallas_call x7 -> x8, Pallas kernels: 10.3 us -> 19.8 us  [merge_call(): pl.pallas_call(functools.partial(merge_kernel, size, tuple((c * (size + M...]
    ppermute x5 -> x2, starting transfers between devices: 9.62 us -> 2.48 us  [the longest x1 2.48 us: local_step(): near_b = lax.ppermute(near_b, 'store', NEAR)]
    ppermute x2, waiting for transfers between devices: 0.01 us -> 6.96 us  [local_step(): far.append(lax.ppermute(pair, 'store', ACROSS))]
    ppermute x5 -> x2, waiting for transfers between devices: 15.1 us -> 21.5 us  [the longest x1 20.3 us: local_step(): near_a = lax.ppermute(near_a, 'store', NEAR)]
  transfers between devices with their start and end apart: 23 -> 21, of which waited for: 7 -> 8; matrix products, arithmetic and copies ran while one was open for 9% -> 10% of each run, Pallas kernels for 34% -> 31%
where the time goes in v2:
time: 322 us; the launch traced here: 321 us
  Pallas kernels  118 us (37%)
  waiting for transfers between devices  110 us (34%)
  starting transfers between devices  55.3 us (17%)
  matrix products  27.4 us (9%)
  other arithmetic  4.69 us (1%)
  local copies, waits for them, and re-layouts  4.62 us (1%)
    pallas_call x3, Pallas kernels, scatter_call(): pl.pallas_call(functools.partial(scatter_kernel, tuple((seg[1:] for seg i...  60 us
    ppermute x11, waiting for transfers between devices, swap(): return lax.ppermute(x, axis, [(i, i ^ bit) for i in range(4)])  49.6 us
    pallas_call x2, Pallas kernels, score_call(): pl.pallas_call(functools.partial(scores_kernel, first, count, bool(prev))...  33.7 us
    ppermute x2, waiting for transfers between devices, local_step(): inward = lax.ppermute(plane, 'store', INWARD)  32 us
    ppermute x2, starting transfers between devices, local_step(): inward = lax.ppermute(plane, 'store', INWARD)  30.3 us
    dot_general x1, matrix products, local_step(): lax.dot_general(my_rows, w_head, (((1,), (0,)), ((), ())), preferred_elem...  27.4 us
    ppermute x1, waiting for transfers between devices, local_step(): near_a = lax.ppermute(near_a, 'store', NEAR)  20.3 us
    pallas_call x8, Pallas kernels, merge_call(): pl.pallas_call(functools.partial(merge_kernel, size, tuple((c * (size + M...  19.8 us
  transfers between devices with their start and end apart: 21, of which 8 were waited for; matrix products, arithmetic and copies ran while one was open for 10% of the time, Pallas kernels for 31%

profile of v2, /device:TPU:0, one launch (start us, length us, event | category | flops | bytes accessed | tf_op | source)
XLA Modules:
  0.0 321.4 jit_solution(510018931628259815)
XLA Ops:
  0.7 13.8 %scores.2 = (f32[4096,128]{1,0:T(8,128)}, f32[1600,128]{1,0:T(8,128)}, f32[1600,128]{1,0:T(8,128)}, f32[4096,128]{1,0:T(8,128)}, s32[64,128]{1,0:T(8,128)}) custom-call(s32[1]{0:T(128)} %bitcast.s_ref, s32[1]{0:T(128)} %bitcast.2.m_ref, f32[1]{0:T(128)} %bitcast.13.tau_ref, bf16[256,4096]{1,0:T(8,128)(2,1)} %q_hbm.3, bf16[8192,4096]{1,0:T(8,128)(2,1)} %k_hbm.3, ...), custom_call_target="tpu_custom_call" | custom-call | flops 6442450944 | bytes 25165824 | tf_op jit(solution)/shard_map/scores/pallas_call | solution.py:136
  14.5 1.6 collective-permute-start.5
  16.1 7.7 %collective-permute-start.4 = (f32[1600,128]{1,0:T(8,128)}, f32[1600,128]{1,0:T(8,128)}, u32[]{:S(2)}, u32[]{:S(2)}) collective-permute-start(f32[1600,128]{1,0:T(8,128)} %get-tuple-element.27), channel_id=1, source_target_pairs={{0,8},{12,4},{1,9},{13,5},{2,10},{14,6},{3,11},{15,7},{16,24},{28,... | collective-permute-start | bytes 2457608 | tf_op jit(solution)/shard_map/ppermute | solution.py:446
  23.7 19.9 %scores.3 = (f32[4096,128]{1,0:T(8,128)}, f32[2560,128]{1,0:T(8,128)}, f32[2560,128]{1,0:T(8,128)}, f32[4096,128]{1,0:T(8,128)}) custom-call(s32[1]{0:T(128)} %bitcast.s_ref, s32[1]{0:T(128)} %bitcast.2.m_ref, f32[1]{0:T(128)} %bitcast.14.tau_ref, bf16[256,4096]{1,0:T(8,128)(2,1)} %q_hbm.3, ...), custom_call_target="tpu_custom_call", output_to_operand_aliasing={{0}: (6, {}), {3}: (7, {})} | custom-call | flops 10737418240 | bytes 41943040 | tf_op jit(solution)/shard_map/scores/pallas_call | solution.py:136
  43.7 2.4 collective-permute-start.7
  46.0 1.7 collective-permute-start.8
  47.7 19.2 %scatter.5 = (f32[4112,128]{1,0:T(8,128)}, f32[4112,128]{1,0:T(8,128)}, f32[4112,128]{1,0:T(8,128)}, f32[4112,128]{1,0:T(8,128)}) custom-call(s32[1]{0:T(128)} %bitcast.s_ref, s32[8192]{0:T(1024)} %bitcast.18, f32[4096,128]{1,0:T(8,128)} %get-tuple-element.42.refs_1_), custom_call_target="tpu_custom_call" | custom-call | flops 8192000000 | bytes 4194304 | tf_op jit(solution)/shard_map/scatter/pallas_call | solution.py:307
  67.0 0.1 collective-permute-start.14
  67.0 1.4 fusion.2.refs_3_.refs_2_
  68.4 0.5 collective-permute-start.13
  68.9 1.4 fusion.3.refs_2_.refs_1_
  70.3 20.3 %collective-permute-done.3.refs_5_ = f32[1600,128]{1,0:T(8,128)} collective-permute-done((f32[1600,128]{1,0:T(8,128)}, f32[1600,128]{1,0:T(8,128)}, u32[]{:S(2)}, u32[]{:S(2)}) %collective-permute-start.3) | collective-permute-done | bytes 819232 | tf_op jit(solution)/shard_map/ppermute | solution.py:448
  90.6 2.5 collective-permute-start.6
  93.1 1.4 fusion.4.refs_1_.refs_0_
  94.5 25.5 %scatter.3 = (f32[4112,128]{1,0:T(8,128)}, f32[4112,128]{1,0:T(8,128)}, f32[4112,128]{1,0:T(8,128)}, f32[4112,128]{1,0:T(8,128)}) custom-call(s32[1]{0:T(128)} %bitcast.s_ref, s32[8192]{0:T(1024)} %bitcast.19, s32[8192]{0:T(1024)} %fusion.4.refs_1_.refs_0_, s32[8192]{0:T(1024)} %fusion.3.refs_2_.refs_1_, s32[8192]{0:T(1024)} %fusion.2.refs_3_.refs_2_, ...), custom_call_target="tpu_custom_call" | custom-call | flops 17408000000 | bytes 8912896 | tf_op jit(solution)/shard_map/scatter/pallas_call | solution.py:307
  120.0 1.1 collective-permute-done.6.refs_3_
  121.1 15.4 %scatter.4 = (f32[4112,128]{1,0:T(8,128)}, f32[4112,128]{1,0:T(8,128)}, f32[4112,128]{1,0:T(8,128)}, f32[4112,128]{1,0:T(8,128)}) custom-call(s32[1]{0:T(128)} %bitcast.s_ref, s32[8192]{0:T(1024)} %fusion.4.refs_1_.refs_0_, s32[8192]{0:T(1024)} %fusion.3.refs_2_.refs_1_, s32[8192]{0:T(1024)} %fusion.2.refs_3_.refs_2_, ...), custom_call_target="tpu_custom_call" | custom-call | flops 15360000000 | bytes 7864320 | tf_op jit(solution)/shard_map/scatter/pallas_call | solution.py:307
  136.6 2.4 merge.13
  139.0 1.6 collective-permute-start.18
  140.5 2.4 merge.10
  142.9 0.6 collective-permute-start.15
  143.5 27.4 %fusion.6 = (f32[64]{0:T(128)S(1)}, f32[64,8000]{1,0:T(8,128)S(1)}) fusion(bf16[4096,8000]{0,1:T(8,128)(2,1)} %param.7, bf16[256,4096]{1,0:T(8,128)(2,1)} %q_hbm.3, s32[]{:T(128)S(6)} %select_n.3), kind=kOutput, calls=%fused_computation.11 | convolution fusion | flops 4194816000 | bytes 68108544 | tf_op jit(solution)/shard_map/dot_general | solution.py:484
  170.9 0.5 exponential_reduce_fusion
  171.4 1.3 copy-done
  172.8 0.1 pad_maximum_fusion.s0_ref
  172.9 1.6 collective-permute-start.1
  174.5 0.1 collective-permute-start.9
  174.6 2.8 merge.14.refs_0_
  177.4 10.5 %collective-permute-done.15.refs_2_ = f32[2056,128]{1,0:T(8,128)} collective-permute-done((f32[2056,128]{1,0:T(8,128)}, f32[2056,128]{1,0:T(8,128)}, u32[]{:S(2)}, u32[]{:S(2)}) %collective-permute-start.15) | collective-permute-done | bytes 1052704 | tf_op jit(solution)/shard_map/ppermute | solution.py:429
  187.9 28.0 %collective-permute-start.19 = (f32[2056,128]{1,0:T(8,128)}, f32[2056,128]{1,0:T(8,128)}, u32[]{:S(2)}, u32[]{:S(2)}) collective-permute-start(f32[2056,128]{1,0:T(8,128)} %merge.14.refs_0_), channel_id=1, source_target_pairs={{0,4},{12,8},{1,5},{13,9},{2,6},{14,10},{3,7},{15,11},{16,20},{28,... | collective-permute-start | bytes 3158024 | tf_op jit(solution)/shard_map/ppermute | solution.py:474
  215.9 2.7 merge.11.refs_0_
  218.7 2.3 collective-permute-start.16
  221.0 2.4 merge.9
  223.3 2.4 merge.8
  225.7 13.1 %collective-permute-done.19.refs_1_ = f32[2056,128]{1,0:T(8,128)} collective-permute-done((f32[2056,128]{1,0:T(8,128)}, f32[2056,128]{1,0:T(8,128)}, u32[]{:S(2)}, u32[]{:S(2)}) %collective-permute-start.19) | collective-permute-done | bytes 1052704 | tf_op jit(solution)/shard_map/ppermute | solution.py:474
  238.8 2.4 merge.15
  241.3 18.9 %collective-permute-done.16.refs_1_ = f32[2056,128]{1,0:T(8,128)} collective-permute-done((f32[2056,128]{1,0:T(8,128)}, f32[2056,128]{1,0:T(8,128)}, u32[]{:S(2)}, u32[]{:S(2)}) %collective-permute-start.16) | collective-permute-done | bytes 1052704 | tf_op jit(solution)/shard_map/ppermute | solution.py:474
  260.1 1.5 collective-permute-start.12
  261.6 2.4 merge.12
  264.0 0.6 collective-permute-start.11
  264.6 1.3 collective-permute-start.20
  265.9 1.3 collective-permute-start.17
  267.9 18.7 %collective-permute-done.12.refs_1_ = f32[2056,128]{1,0:T(8,128)} collective-permute-done((f32[2056,128]{1,0:T(8,128)}, f32[2056,128]{1,0:T(8,128)}, u32[]{:S(2)}, u32[]{:S(2)}) %collective-permute-start.12) | collective-permute-done | bytes 1052704 | tf_op jit(solution)/shard_map/ppermute | solution.py:429
  286.6 20.3 %collective-permute-done.11.refs_0_ = f32[2056,128]{1,0:T(8,128)S(1)} collective-permute-done((f32[2056,128]{1,0:T(8,128)}, f32[2056,128]{1,0:T(8,128)S(1)}, u32[]{:S(2)}, u32[]{:S(2)}) %collective-permute-start.11) | collective-permute-done | bytes 1052704 | tf_op jit(solution)/shard_map/ppermute | solution.py:429
  306.9 7.0 %collective-permute-done.17.refs_2_ = f32[2056,128]{1,0:T(8,128)S(1)} collective-permute-done((f32[2056,128]{1,0:T(8,128)}, f32[2056,128]{1,0:T(8,128)S(1)}, u32[]{:S(2)}, u32[]{:S(2)}) %collective-permute-start.17) | collective-permute-done | bytes 1052704 | tf_op jit(solution)/shard_map/ppermute | solution.py:476
  313.9 1.6 copy-done.1
  315.5 1.6 copy-done.2
  317.0 4.3 %final.1 = f32[64,8000]{1,0:T(8,128)} custom-call(s32[1]{0:T(128)} %bitcast.s_ref, f32[1]{0:T(128)} %bitcast.15.mix_ref, f32[64,8000]{1,0:T(8,128)S(1)} %copy-done.1, f32[64,128]{1,0:T(8,128)S(1)} %pad_maximum_fusion.s0_ref, f32[64,128]{1,0:T(8,128)S(1)} %collective-permute-done.s1_ref, f32[64,128]{1,0:T(8,128)S(1)} %collective-permute-done.1.s2_ref, ...), custom_call_target="tpu_custom_call" | custom-call | flops 5000000000 | bytes 12582912 | tf_op jit(solution)/shard_map/final/pallas_call | solution.py:406
  (22 shorter events, 0.3 us)
Async XLA Ops:
  14.5 52.5 %collective-permute-start.5 = (f32[1600,128]{1,0:T(8,128)}, f32[1600,128]{1,0:T(8,128)}, u32[]{:S(2)}, u32[]{:S(2)}) collective-permute-start(f32[1600,128]{1,0:T(8,128)} %get-tuple-element.27), channel_id=1, source_target_pairs={{4,8},{8,4},{5,9},{9,5},{6,10},{10,6},{7,11},{11,7},{20,24},{24,20... | collective-permute-start | bytes 2457608 | tf_op jit(solution)/shard_map/ppermute | solution.py:447
  16.1 52.3 %collective-permute-start.4 = (f32[1600,128]{1,0:T(8,128)}, f32[1600,128]{1,0:T(8,128)}, u32[]{:S(2)}, u32[]{:S(2)}) collective-permute-start(f32[1600,128]{1,0:T(8,128)} %get-tuple-element.27), channel_id=1, source_target_pairs={{0,8},{12,4},{1,9},{13,5},{2,10},{14,6},{3,11},{15,7},{16,24},{28,... | collective-permute-start | bytes 2457608 | tf_op jit(solution)/shard_map/ppermute | solution.py:446
  43.7 76.3 %collective-permute-start.7 = (f32[2560,128]{1,0:T(8,128)}, f32[2560,128]{1,0:T(8,128)}, u32[]{:S(2)}, u32[]{:S(2)}) collective-permute-start(f32[2560,128]{1,0:T(8,128)} %get-tuple-element.31), channel_id=1, source_target_pairs={{0,8},{12,4},{1,9},{13,5},{2,10},{14,6},{3,11},{15,7},{16,24},{28,... | collective-permute-start | bytes 3932168 | tf_op jit(solution)/shard_map/ppermute | solution.py:450
  46.0 73.9 %collective-permute-start.8 = (f32[2560,128]{1,0:T(8,128)}, f32[2560,128]{1,0:T(8,128)}, u32[]{:S(2)}, u32[]{:S(2)}) collective-permute-start(f32[2560,128]{1,0:T(8,128)} %get-tuple-element.31), channel_id=1, source_target_pairs={{4,8},{8,4},{5,9},{9,5},{6,10},{10,6},{7,11},{11,7},{20,24},{24,20... | collective-permute-start | bytes 3932168 | tf_op jit(solution)/shard_map/ppermute | solution.py:451
  47.7 42.9 %collective-permute-start.3 = (f32[1600,128]{1,0:T(8,128)}, f32[1600,128]{1,0:T(8,128)}, u32[]{:S(2)}, u32[]{:S(2)}) collective-permute-start(f32[1600,128]{1,0:T(8,128)} %get-tuple-element.26), channel_id=1, source_target_pairs={{0,4},{4,0},{8,12},{12,8},{1,5},{5,1},{9,13},{13,9},{2,6},{6,2},{1... | collective-permute-start | bytes 2457608 | tf_op jit(solution)/shard_map/ppermute | solution.py:448
  67.0 69.6 %collective-permute-start.14 = (f32[4112,128]{1,0:T(8,128)}, f32[4112,128]{1,0:T(8,128)}, u32[]{:S(2)}, u32[]{:S(2)}) collective-permute-start(f32[4112,128]{1,0:T(8,128)} %get-tuple-element.46), channel_id=1, source_target_pairs={{0,1},{1,0},{2,3},{3,2},{4,5},{5,4},{6,7},{7,6},{8,9},{9,8},{10,11... | collective-permute-start | bytes 6316040 | tf_op jit(solution)/shard_map/ppermute | solution.py:429
  68.4 104.5 %collective-permute-start.13 = (f32[4112,128]{1,0:T(8,128)}, f32[4112,128]{1,0:T(8,128)}, u32[]{:S(2)}, u32[]{:S(2)}) collective-permute-start(f32[4112,128]{1,0:T(8,128)} %get-tuple-element.44), channel_id=1, source_target_pairs={{0,1},{1,0},{2,3},{3,2},{4,5},{5,4},{6,7},{7,6},{8,9},{9,8},{10,11... | collective-permute-start | bytes 6316040 | tf_op jit(solution)/shard_map/ppermute | solution.py:429
  90.6 30.5 %collective-permute-start.6 = (f32[2560,128]{1,0:T(8,128)}, f32[2560,128]{1,0:T(8,128)}, u32[]{:S(2)}, u32[]{:S(2)}) collective-permute-start(f32[2560,128]{1,0:T(8,128)} %get-tuple-element.30), channel_id=1, source_target_pairs={{0,4},{4,0},{8,12},{12,8},{1,5},{5,1},{9,13},{13,9},{2,6},{6,2},{1... | collective-permute-start | bytes 3932168 | tf_op jit(solution)/shard_map/ppermute | solution.py:452
  136.5 82.2 %collective-permute-start.10 = (f32[4112,128]{1,0:T(8,128)}, f32[4112,128]{1,0:T(8,128)}, u32[]{:S(2)}, u32[]{:S(2)}) collective-permute-start(f32[4112,128]{1,0:T(8,128)} %get-tuple-element.41), channel_id=1, source_target_pairs={{0,1},{1,0},{2,3},{3,2},{4,5},{5,4},{6,7},{7,6},{8,9},{9,8},{10,11... | collective-permute-start | bytes 6316040 | tf_op jit(solution)/shard_map/ppermute | solution.py:429
  139.0 35.5 %collective-permute-start.18 = (f32[2056,128]{1,0:T(8,128)}, f32[2056,128]{1,0:T(8,128)}, u32[]{:S(2)}, u32[]{:S(2)}) collective-permute-start(f32[2056,128]{1,0:T(8,128)} %merge.13), channel_id=1, source_target_pairs={{0,2},{1,3},{2,0},{3,1},{4,6},{5,7},{6,4},{7,5},{8,10},{9,11},{10,... | collective-permute-start | bytes 3158024 | tf_op jit(solution)/shard_map/ppermute | solution.py:429
  142.9 45.0 %collective-permute-start.15 = (f32[2056,128]{1,0:T(8,128)}, f32[2056,128]{1,0:T(8,128)}, u32[]{:S(2)}, u32[]{:S(2)}) collective-permute-start(f32[2056,128]{1,0:T(8,128)} %merge.10), channel_id=1, source_target_pairs={{0,2},{1,3},{2,0},{3,1},{4,6},{5,7},{6,4},{7,5},{8,10},{9,11},{10,... | collective-permute-start | bytes 3158024 | tf_op jit(solution)/shard_map/ppermute | solution.py:429
  171.3 1.3 copy-start
  172.9 91.1 %collective-permute-start = (f32[64,128]{1,0:T(8,128)S(1)}, f32[64,128]{1,0:T(8,128)S(1)}, u32[]{:S(2)}, u32[]{:S(2)}) collective-permute-start(f32[64,128]{1,0:T(8,128)S(1)} %pad_maximum_fusion.s0_ref), channel_id=1, source_target_pairs={{0,1},{1,0},{2,3},{3,2},{4,5},{5,4},{6,7},{7,6},{8,9},{9,8},{10,11... | collective-permute-start | bytes 98312 | tf_op jit(solution)/shard_map/ppermute | solution.py:429
  172.9 91.7 %collective-permute-start.1 = (f32[64,128]{1,0:T(8,128)S(1)}, f32[64,128]{1,0:T(8,128)S(1)}, u32[]{:S(2)}, u32[]{:S(2)}) collective-permute-start(f32[64,128]{1,0:T(8,128)S(1)} %pad_maximum_fusion.s0_ref), channel_id=1, source_target_pairs={{0,2},{1,3},{2,0},{3,1},{4,6},{5,7},{6,4},{7,5},{8,10},{9,11},{10,... | collective-permute-start | bytes 98312 | tf_op jit(solution)/shard_map/ppermute | solution.py:429
  174.5 93.4 %collective-permute-start.9 = (f32[4112,128]{1,0:T(8,128)}, f32[4112,128]{1,0:T(8,128)}, u32[]{:S(2)}, u32[]{:S(2)}) collective-permute-start(f32[4112,128]{1,0:T(8,128)} %get-tuple-element.39), channel_id=1, source_target_pairs={{0,1},{1,0},{2,3},{3,2},{4,5},{5,4},{6,7},{7,6},{8,9},{9,8},{10,11... | collective-permute-start | bytes 6316040 | tf_op jit(solution)/shard_map/ppermute | solution.py:429
  187.9 50.9 %collective-permute-start.19 = (f32[2056,128]{1,0:T(8,128)}, f32[2056,128]{1,0:T(8,128)}, u32[]{:S(2)}, u32[]{:S(2)}) collective-permute-start(f32[2056,128]{1,0:T(8,128)} %merge.14.refs_0_), channel_id=1, source_target_pairs={{0,4},{12,8},{1,5},{13,9},{2,6},{14,10},{3,7},{15,11},{16,20},{28,... | collective-permute-start | bytes 3158024 | tf_op jit(solution)/shard_map/ppermute | solution.py:474
  218.7 41.5 %collective-permute-start.16 = (f32[2056,128]{1,0:T(8,128)}, f32[2056,128]{1,0:T(8,128)}, u32[]{:S(2)}, u32[]{:S(2)}) collective-permute-start(f32[2056,128]{1,0:T(8,128)} %merge.11.refs_0_), channel_id=1, source_target_pairs={{0,4},{12,8},{1,5},{13,9},{2,6},{14,10},{3,7},{15,11},{16,20},{28,... | collective-permute-start | bytes 3158024 | tf_op jit(solution)/shard_map/ppermute | solution.py:474
  238.8 27.1 %collective-permute-start.2 = (f32[64,128]{1,0:T(8,128)S(1)}, f32[64,128]{1,0:T(8,128)S(1)}, u32[]{:S(2)}, u32[]{:S(2)}) collective-permute-start(f32[64,128]{1,0:T(8,128)S(1)} %pad_maximum_fusion.s0_ref), channel_id=1, source_target_pairs={{0,3},{1,2},{2,1},{3,0},{4,7},{5,6},{6,5},{7,4},{8,11},{9,10},{10,... | collective-permute-start | bytes 98312 | tf_op jit(solution)/shard_map/ppermute | solution.py:429
  260.1 26.4 %collective-permute-start.12 = (f32[2056,128]{1,0:T(8,128)}, f32[2056,128]{1,0:T(8,128)}, u32[]{:S(2)}, u32[]{:S(2)}) collective-permute-start(f32[2056,128]{1,0:T(8,128)} %merge.9), channel_id=1, source_target_pairs={{0,2},{1,3},{2,0},{3,1},{4,6},{5,7},{6,4},{7,5},{8,10},{9,11},{10,... | collective-permute-start | bytes 3158024 | tf_op jit(solution)/shard_map/ppermute | solution.py:429
  264.0 42.9 %collective-permute-start.11 = (f32[2056,128]{1,0:T(8,128)}, f32[2056,128]{1,0:T(8,128)S(1)}, u32[]{:S(2)}, u32[]{:S(2)}) collective-permute-start(f32[2056,128]{1,0:T(8,128)} %merge.8), channel_id=1, source_target_pairs={{0,2},{1,3},{2,0},{3,1},{4,6},{5,7},{6,4},{7,5},{8,10},{9,11},{10,... | collective-permute-start | bytes 3158024 | tf_op jit(solution)/shard_map/ppermute | solution.py:429
  264.6 42.3 %collective-permute-start.20 = (f32[2056,128]{1,0:T(8,128)}, f32[2056,128]{1,0:T(8,128)S(1)}, u32[]{:S(2)}, u32[]{:S(2)}) collective-permute-start(f32[2056,128]{1,0:T(8,128)} %merge.15), channel_id=1, source_target_pairs={{4,12},{8,0},{5,13},{9,1},{6,14},{10,2},{7,15},{11,3},{20,28},{24,... | collective-permute-start | bytes 3158024 | tf_op jit(solution)/shard_map/ppermute | solution.py:476
  265.9 48.0 %collective-permute-start.17 = (f32[2056,128]{1,0:T(8,128)}, f32[2056,128]{1,0:T(8,128)S(1)}, u32[]{:S(2)}, u32[]{:S(2)}) collective-permute-start(f32[2056,128]{1,0:T(8,128)} %merge.12), channel_id=1, source_target_pairs={{4,12},{8,0},{5,13},{9,1},{6,14},{10,2},{7,15},{11,3},{20,28},{24,... | collective-permute-start | bytes 3158024 | tf_op jit(solution)/shard_map/ppermute | solution.py:476
  313.9 1.6 copy-start.1
  315.5 1.6 copy-start.2

commit v3 on v2

--- a/solution.py
+++ b/solution.py
@@ -14,7 +14,7 @@
 WIDE = 2
 VOCAB_LOC = 8000
 PIECE = 4096
-FIRST = 6
+FIRST = 8
 META = 8
 SLOTS = 4
 OUT_GROUP = 2
@@ -157,6 +157,37 @@
     )(me, model, tau, queries, keys, tok2, *prev)
 
 
+def ids_kernel(*refs):
+    n = len(refs) - 5
+    srcs, (out_hbm, raw, ids, sem, out_sem) = refs[:n], refs[n:]
+    loads = [pltpu.make_async_copy(r.at[pl.ds(r.shape[0] - TOK_ROWS, TOK_ROWS)], raw.at[i], sem.at[i]) for i, r in enumerate(srcs)]
+    saves = [pltpu.make_async_copy(ids.at[i], out_hbm.at[pl.ds(i * TOK_ROWS, TOK_ROWS)], out_sem.at[i]) for i in range(n)]
+    for load in loads:
+        load.start()
+    for i in range(n):
+        loads[i].wait()
+        ids[i] = raw[i].astype(jnp.int32)
+        saves[i].start()
+    for save in saves:
+        save.wait()
+
+
+def ids_call(arrays):
+    n = len(arrays)
+    hbm = pl.BlockSpec(memory_space=pltpu.HBM)
+    shape = (n, TOK_ROWS, LANES)
+    return pl.pallas_call(
+        ids_kernel,
+        in_specs=[hbm] * n,
+        out_specs=hbm,
+        out_shape=jax.ShapeDtypeStruct((n * TOK_ROWS, LANES), jnp.int32),
+        scratch_shapes=[pltpu.VMEM(shape, jnp.float32), pltpu.VMEM(shape, jnp.int32), pltpu.SemaphoreType.DMA((n,)), pltpu.SemaphoreType.DMA((n,))],
+        compiler_params=pltpu.CompilerParams(vmem_limit_bytes=VMEM),
+        cost_estimate=pl.CostEstimate(flops=1_000_000, bytes_accessed=1 << 18, transcendentals=0),
+        name="ids",
+    )(*arrays)
+
+
 def fold(row, op):
     wide = jnp.broadcast_to(row, (8, LANES))
     return op(wide, pltpu.roll(wide, 64, 1))[:1]
@@ -327,45 +358,56 @@
     )(s1, *codes, *xs, *(prev if carried else ()))
 
 
-def merge_kernel(size, offsets, *refs):
-    n = len(offsets)
-    srcs, out_hbm, (stage, sem, out_sem, *bufs) = refs[:n], refs[n], refs[n + 1:]
+def merge_kernel(size, groups, *refs):
+    n, n_out = len(groups[0]), len(groups)
+    srcs, outs, refs = refs[:n], refs[n:n + n_out], refs[n + n_out:]
+    stages, sem, out_sem, bufs = refs[:n_out], refs[n_out], refs[n_out + 1], refs[n_out + 2:]
     step = size // MERGE_STEPS
     parts = [(size, META)] + [(i * step, step) for i in range(MERGE_STEPS)]
-    loads = [[pltpu.make_async_copy(r.at[pl.ds(o + at, rows)], b.at[pl.ds(at, rows)], sem.at[i, j]) for i, (r, o, b) in enumerate(zip(srcs, offsets, bufs))] for j, (at, rows) in enumerate(parts)]
-    saves = [pltpu.make_async_copy(stage.at[pl.ds(at, rows)], out_hbm.at[pl.ds(at, rows)], out_sem.at[j]) for j, (at, rows) in enumerate(parts)]
-    for group in loads:
-        for load in group:
-            load.start()
-    for j, (at, rows) in enumerate(parts):
-        for load in loads[j]:
-            load.wait()
-        if j == 0:
-            tops = [b[size + 1:size + 2, :] for b in bufs]
-            top = functools.reduce(jnp.maximum, tops)
-            scales = [jnp.exp(t - top) for t in tops]
-        total = functools.reduce(jnp.add, [b[at:at + rows, :] * f for b, f in zip(bufs, scales)])
-        if j == 0:
-            total = jnp.where(lax.broadcasted_iota(jnp.int32, (META, LANES), 0) == 1, top, total)
-        stage[at:at + rows, :] = total
-        saves[j].start()
-    for save in saves:
-        save.wait()
-
-
-def merge_call(size, parts):
+    work = []
+    for g, offsets in enumerate(groups):
+        mine = bufs[g * n:g * n + n]
+        loads = [[pltpu.make_async_copy(r.at[pl.ds(o + at, rows)], b.at[pl.ds(at, rows)], sem.at[g, i, j]) for i, (r, o, b) in enumerate(zip(srcs, offsets, mine))] for j, (at, rows) in enumerate(parts)]
+        saves = [pltpu.make_async_copy(stages[g].at[pl.ds(at, rows)], outs[g].at[pl.ds(at, rows)], out_sem.at[g, j]) for j, (at, rows) in enumerate(parts)]
+        work.append((mine, loads, saves, stages[g]))
+    for _, loads, _, _ in work:
+        for group in loads:
+            for load in group:
+                load.start()
+    for mine, loads, saves, stage in work:
+        for j, (at, rows) in enumerate(parts):
+            for load in loads[j]:
+                load.wait()
+            if j == 0:
+                tops = [b[size + 1:size + 2, :] for b in mine]
+                top = functools.reduce(jnp.maximum, tops)
+                scales = [jnp.exp(t - top) for t in tops]
+            total = functools.reduce(jnp.add, [b[at:at + rows, :] * f for b, f in zip(mine, scales)])
+            if j == 0:
+                total = jnp.where(lax.broadcasted_iota(jnp.int32, (META, LANES), 0) == 1, top, total)
+            stage[at:at + rows, :] = total
+            saves[j].start()
+    for _, _, saves, _ in work:
+        for save in saves:
+            save.wait()
+
+
+def merge_call(size, arrays, groups):
     hbm = pl.BlockSpec(memory_space=pltpu.HBM)
     shape = (size + META, LANES)
+    n, n_out = len(arrays), len(groups)
     return pl.pallas_call(
-        functools.partial(merge_kernel, size, tuple(c * (size + META) for _, c in parts)),
-        in_specs=[hbm] * len(parts),
-        out_specs=hbm,
-        out_shape=jax.ShapeDtypeStruct(shape, jnp.float32),
-        scratch_shapes=[pltpu.VMEM(shape, jnp.float32), pltpu.SemaphoreType.DMA((len(parts), MERGE_STEPS + 1)), pltpu.SemaphoreType.DMA((MERGE_STEPS + 1,))] + [pltpu.VMEM(shape, jnp.float32)] * len(parts),
+        functools.partial(merge_kernel, size, tuple(tuple(c * (size + META) for c in group) for group in groups)),
+        in_specs=[hbm] * n,
+        out_specs=[hbm] * n_out,
+        out_shape=[jax.ShapeDtypeStruct(shape, jnp.float32)] * n_out,
+        scratch_shapes=[pltpu.VMEM(shape, jnp.float32)] * n_out
+        + [pltpu.SemaphoreType.DMA((n_out, n, MERGE_STEPS + 1)), pltpu.SemaphoreType.DMA((n_out, MERGE_STEPS + 1))]
+        + [pltpu.VMEM(shape, jnp.float32)] * (n * n_out),
         compiler_params=pltpu.CompilerParams(vmem_limit_bytes=VMEM),
-        cost_estimate=pl.CostEstimate(flops=4_000_000_000, bytes_accessed=size * 2048, transcendentals=0),
+        cost_estimate=pl.CostEstimate(flops=4_000_000_000, bytes_accessed=size * 2048 * n_out, transcendentals=0),
         name="merge",
-    )(*[a for a, _ in parts])
+    )(*arrays)
 
 
 def final_kernel(chunks, s_ref, mix_ref, logits_ref, s0_ref, s1_ref, s2_ref, s3_ref, keep_ref, mate_ref, *refs):
@@ -451,33 +493,32 @@
         far1_b = lax.ppermute(sparse_b, "store", FAR1)
         near_b = lax.ppermute(near_b, "store", NEAR)
         code_own = code_own.reshape(-1)
-        code_far2, code_far1, code_near = [x[-TOK_ROWS:].astype(jnp.int32).reshape(-1) for x in (far2_a, far1_a, near_a)]
+        codes = ids_call([near_a, far2_a, far1_a]).reshape(-1)
+        n_all = n_a + 2 * rows_b
 
         dense = scatter_call(s1, [code_own], [dense], ((rows_a + rows_b, 0, 0, False),), None)
         d_next = swap(dense[3], "model", 1)
         d_mate = swap(dense[1], "model", 1)
-        d_y = []
-        for c in range(CHUNKS):
-            part = merge_call(size, [(dense[2], c), (d_next, c)])
-            d_y.append(swap(part, "model", 2))
-
-        segments = ((rows_a + rows_b, 0, 0, False), (rows_a, 1, 0, False), (rows_a, 2, 0, True), (rows_a, 3, 0, True))
-        part = scatter_call(s1, [code_own, code_near, code_far2, code_far1], [own, near_a, far2_a, far1_a], segments, None)
-        segments = ((rows_b, 0, n_a, False), (rows_b, 1, n_a, True), (rows_b, 2, n_a, True))
-        keep, mate, ynext, matey = scatter_call(s1, [code_near, code_far2, code_far1], [near_b, far2_b, far1_b], segments, part)
+        parts = merge_call(size, [dense[2], d_next], [(c, c) for c in range(CHUNKS)])
+        d_y = [swap(parts[c], "model", 2) for c in range(CHUNKS)]
+
+        segments = ((rows_a + rows_b, 0, 0, False), (rows_a, 1, 0, False), (rows_a, 1, n_all, True), (rows_a, 1, 2 * n_all, True))
+        part = scatter_call(s1, [code_own, codes], [own, near_a, far2_a, far1_a], segments, None)
+        segments = ((rows_b, 0, n_a, False), (rows_b, 0, n_all + n_a, True), (rows_b, 0, 2 * n_all + n_a, True))
+        keep, mate, ynext, matey = scatter_call(s1, [codes], [near_b, far2_b, far1_b], segments, part)
         matey = swap(matey, "model", 1)
         mate = swap(mate, "model", 1)
 
         far = []
         for c in range(CHUNKS):
-            plane = merge_call(size, [(dense[0], c), (d_mate, c), (d_y[c], 0)])
+            plane, = merge_call(size, [dense[0], d_mate, d_y[c]], [(c, c, 0)])
             inward = lax.ppermute(plane, "store", INWARD)
-            pair = merge_call(size, [(plane, 0), (inward, 0)])
+            pair, = merge_call(size, [plane, inward], [(0, 0)])
             far.append(lax.ppermute(pair, "store", ACROSS))
 
         from_y = []
         for c in range(CHUNKS):
-            part = merge_call(size, [(ynext, c), (matey, c)])
+            part, = merge_call(size, [ynext, matey], [(c, c)])
             from_y.append(swap(part, "model", 2))
 
         my_rows = lax.dynamic_slice_in_dim(queries, s * rows_loc, rows_loc, axis=0)

time: 322 us -> 307 us (0.953)
  starting transfers between devices: 55.3 us -> 48 us
  other arithmetic: 4.69 us -> 0.57 us
  waiting for transfers between devices: 110 us -> 106 us
    ppermute x1, waiting for transfers between devices: 20.3 us -> 2.02 us  [local_step(): near_a = lax.ppermute(near_a, 'store', NEAR)]
    ppermute x1, waiting for transfers between devices: 1.15 us -> 12.9 us  [local_step(): near_b = lax.ppermute(near_b, 'store', NEAR)]
    ppermute x2, starting transfers between devices: 30.3 us -> 21.3 us  [local_step(): inward = lax.ppermute(plane, 'store', INWARD)]
    reshape x3 -> x0, other arithmetic: 4.12 us -> none  [local_step(): x[-TOK_ROWS:].astype(jnp.int32).reshape(-1)]
  transfers between devices with their start and end apart: 21 -> 21, of which waited for: 8 -> 8; matrix products, arithmetic and copies ran while one was open for 10% -> 9% of each run, Pallas kernels for 31% -> 32%
where the time goes in v3:
time: 307 us; the launch traced here: 306 us
  Pallas kernels  119 us (39%)
  waiting for transfers between devices  106 us (35%)
  starting transfers between devices  48 us (16%)
  matrix products  27.4 us (9%)
  local copies, waits for them, and re-layouts  4.62 us (2%)
    pallas_call x3, Pallas kernels, scatter_call(): pl.pallas_call(functools.partial(scatter_kernel, tuple((seg[1:] for seg i...  60.6 us
    ppermute x11, waiting for transfers between devices, swap(): return lax.ppermute(x, axis, [(i, i ^ bit) for i in range(4)])  52 us
    pallas_call x2, Pallas kernels, score_call(): pl.pallas_call(functools.partial(scores_kernel, first, count, bool(prev))...  33.8 us
    ppermute x2, waiting for transfers between devices, local_step(): inward = lax.ppermute(plane, 'store', INWARD)  32.1 us
    dot_general x1, matrix products, local_step(): lax.dot_general(my_rows, w_head, (((1,), (0,)), ((), ())), preferred_elem...  27.4 us
    ppermute x2, starting transfers between devices, local_step(): inward = lax.ppermute(plane, 'store', INWARD)  21.3 us
    pallas_call x7, Pallas kernels, merge_call(): pl.pallas_call(functools.partial(merge_kernel, size, tuple((tuple((c * (s...  18.4 us
    ppermute x1, waiting for transfers between devices, local_step(): near_b = lax.ppermute(near_b, 'store', NEAR)  12.9 us
  transfers between devices with their start and end apart: 21, of which 8 were waited for; matrix products, arithmetic and copies ran while one was open for 9% of the time, Pallas kernels for 32%

profile of v3, /device:TPU:0, one launch (start us, length us, event | category | flops | bytes accessed | tf_op | source)
XLA Modules:
  0.0 306.5 jit_solution(11554336838022891060)
XLA Ops:
  0.7 16.9 %scores.2 = (f32[4096,128]{1,0:T(8,128)}, f32[2112,128]{1,0:T(8,128)}, f32[2112,128]{1,0:T(8,128)}, f32[4096,128]{1,0:T(8,128)}, s32[64,128]{1,0:T(8,128)}) custom-call(s32[1]{0:T(128)} %bitcast.s_ref, s32[1]{0:T(128)} %bitcast.2.m_ref, f32[1]{0:T(128)} %bitcast.8.tau_ref, bf16[256,4096]{1,0:T(8,128)(2,1)} %q_hbm.3, bf16[8192,4096]{1,0:T(8,128)(2,1)} %k_hbm.3, ...), custom_call_target="tpu_custom_call" | custom-call | flops 8589934592 | bytes 33554432 | tf_op jit(solution)/shard_map/scores/pallas_call | solution.py:136
  17.5 7.0 %collective-permute-start.4 = (f32[2112,128]{1,0:T(8,128)}, f32[2112,128]{1,0:T(8,128)}, u32[]{:S(2)}, u32[]{:S(2)}) collective-permute-start(f32[2112,128]{1,0:T(8,128)} %get-tuple-element.29), channel_id=1, source_target_pairs={{0,8},{12,4},{1,9},{13,5},{2,10},{14,6},{3,11},{15,7},{16,24},{28,... | collective-permute-start | bytes 3244040 | tf_op jit(solution)/shard_map/ppermute | solution.py:488
  24.5 1.7 collective-permute-start.5
  26.2 16.9 %scores.3 = (f32[4096,128]{1,0:T(8,128)}, f32[2048,128]{1,0:T(8,128)}, f32[2048,128]{1,0:T(8,128)}, f32[4096,128]{1,0:T(8,128)}) custom-call(s32[1]{0:T(128)} %bitcast.s_ref, s32[1]{0:T(128)} %bitcast.2.m_ref, f32[1]{0:T(128)} %bitcast.9.tau_ref, bf16[256,4096]{1,0:T(8,128)(2,1)} %q_hbm.3, ...), custom_call_target="tpu_custom_call", output_to_operand_aliasing={{0}: (6, {}), {3}: (7, {})} | custom-call | flops 8589934592 | bytes 33554432 | tf_op jit(solution)/shard_map/scores/pallas_call | solution.py:136
  43.1 4.8 %collective-permute-start.7 = (f32[2048,128]{1,0:T(8,128)}, f32[2048,128]{1,0:T(8,128)}, u32[]{:S(2)}, u32[]{:S(2)}) collective-permute-start(f32[2048,128]{1,0:T(8,128)} %get-tuple-element.33), channel_id=1, source_target_pairs={{0,8},{12,4},{1,9},{13,5},{2,10},{14,6},{3,11},{15,7},{16,24},{28,... | collective-permute-start | bytes 3145736 | tf_op jit(solution)/shard_map/ppermute | solution.py:492
  47.9 1.6 collective-permute-start.8
  49.5 19.1 %scatter.5 = (f32[4112,128]{1,0:T(8,128)}, f32[4112,128]{1,0:T(8,128)}, f32[4112,128]{1,0:T(8,128)}, f32[4112,128]{1,0:T(8,128)}) custom-call(s32[1]{0:T(128)} %bitcast.s_ref, s32[8192]{0:T(1024)} %bitcast.15, f32[4096,128]{1,0:T(8,128)} %get-tuple-element.44.refs_1_), custom_call_target="tpu_custom_call" | custom-call | flops 8192000000 | bytes 4194304 | tf_op jit(solution)/shard_map/scatter/pallas_call | solution.py:338
  68.7 0.1 collective-permute-start.14
  68.8 0.5 collective-permute-start.13
  69.3 2.0 collective-permute-done.3.refs_0_.refs_3_
  71.3 2.5 collective-permute-start.6
  73.8 1.5 ids.1
  75.2 27.0 %scatter.3 = (f32[4112,128]{1,0:T(8,128)}, f32[4112,128]{1,0:T(8,128)}, f32[4112,128]{1,0:T(8,128)}, f32[4112,128]{1,0:T(8,128)}) custom-call(s32[1]{0:T(128)} %bitcast.s_ref, s32[8192]{0:T(1024)} %bitcast.16, s32[24576]{0:T(1024)} %bitcast.13, f32[4096,128]{1,0:T(8,128)} %get-tuple-element.35.refs_2_, f32[2112,128]{1,0:T(8,128)} %collective-permute-done.3.refs_0_.refs_3_, ...), custom_call_target="tpu_custom_call" | custom-call | flops 20480000000 | bytes 10485760 | tf_op jit(solution)/shard_map/scatter/pallas_call | solution.py:338
  102.3 12.9 %collective-permute-done.6.refs_1_ = f32[2048,128]{1,0:T(8,128)} collective-permute-done((f32[2048,128]{1,0:T(8,128)}, f32[2048,128]{1,0:T(8,128)}, u32[]{:S(2)}, u32[]{:S(2)}) %collective-permute-start.6) | collective-permute-done | bytes 1048608 | tf_op jit(solution)/shard_map/ppermute | solution.py:494
  115.1 14.5 %scatter.4 = (f32[4112,128]{1,0:T(8,128)}, f32[4112,128]{1,0:T(8,128)}, f32[4112,128]{1,0:T(8,128)}, f32[4112,128]{1,0:T(8,128)}) custom-call(s32[1]{0:T(128)} %bitcast.s_ref, s32[24576]{0:T(1024)} %bitcast.14, f32[2048,128]{1,0:T(8,128)} %collective-permute-done.6.refs_1_, f32[2048,128]{1,0:T(8,128)} %collective-permute-done.7.refs_2_, ...), custom_call_target="tpu_custom_call" | custom-call | flops 12288000000 | bytes 6291456 | tf_op jit(solution)/shard_map/scatter/pallas_call | solution.py:338
  129.6 0.1 collective-permute-start.10
  129.7 3.4 %merge.9 = (f32[2056,128]{1,0:T(8,128)}, f32[2056,128]{1,0:T(8,128)}) custom-call(f32[4112,128]{1,0:T(8,128)} %get-tuple-element.47.refs_0_, f32[4112,128]{1,0:T(8,128)} %collective-permute-done.14.refs_1_), custom_call_target="tpu_custom_call" | custom-call | flops 4000000000 | bytes 8388608 | tf_op jit(solution)/shard_map/merge/pallas_call | solution.py:399
  133.2 1.6 collective-permute-start.18
  134.8 0.5 collective-permute-start.15
  135.3 27.4 %fusion.3 = (f32[64]{0:T(128)S(1)}, f32[64,8000]{1,0:T(8,128)S(1)}) fusion(bf16[4096,8000]{0,1:T(8,128)(2,1)} %param.7, bf16[256,4096]{1,0:T(8,128)(2,1)} %q_hbm.3, s32[]{:T(128)S(6)} %select_n.3), kind=kOutput, calls=%fused_computation.5 | convolution fusion | flops 4194816000 | bytes 68108544 | tf_op jit(solution)/shard_map/dot_general | solution.py:525
  162.6 0.5 exponential_reduce_fusion
  163.1 1.3 copy-done
  164.4 0.1 broadcast_in_dim.5
  164.5 0.1 broadcast_in_dim.4
  164.6 0.1 pad_maximum_fusion.s0_ref
  164.7 1.6 collective-permute-start.1
  166.3 0.1 collective-permute-start.9
  166.4 2.8 merge.12.refs_0_
  169.2 12.9 %collective-permute-done.15.refs_2_ = f32[2056,128]{1,0:T(8,128)} collective-permute-done((f32[2056,128]{1,0:T(8,128)}, f32[2056,128]{1,0:T(8,128)}, u32[]{:S(2)}, u32[]{:S(2)}) %collective-permute-start.15) | collective-permute-done | bytes 1052704 | tf_op jit(solution)/shard_map/ppermute | solution.py:471
  182.1 19.0 %collective-permute-start.19 = (f32[2056,128]{1,0:T(8,128)}, f32[2056,128]{1,0:T(8,128)}, u32[]{:S(2)}, u32[]{:S(2)}) collective-permute-start(f32[2056,128]{1,0:T(8,128)} %merge.12.refs_0_), channel_id=1, source_target_pairs={{0,4},{12,8},{1,5},{13,9},{2,6},{14,10},{3,7},{15,11},{16,20},{28,... | collective-permute-start | bytes 3158024 | tf_op jit(solution)/shard_map/ppermute | solution.py:515
  201.1 2.7 merge.10.refs_0_
  203.9 2.3 collective-permute-start.16
  206.2 2.4 merge.8
  208.5 2.4 merge.7
  210.9 13.2 %collective-permute-done.19.refs_1_ = f32[2056,128]{1,0:T(8,128)} collective-permute-done((f32[2056,128]{1,0:T(8,128)}, f32[2056,128]{1,0:T(8,128)}, u32[]{:S(2)}, u32[]{:S(2)}) %collective-permute-start.19) | collective-permute-done | bytes 1052704 | tf_op jit(solution)/shard_map/ppermute | solution.py:515
  224.1 2.4 merge.13
  226.5 19.0 %collective-permute-done.16.refs_1_ = f32[2056,128]{1,0:T(8,128)} collective-permute-done((f32[2056,128]{1,0:T(8,128)}, f32[2056,128]{1,0:T(8,128)}, u32[]{:S(2)}, u32[]{:S(2)}) %collective-permute-start.16) | collective-permute-done | bytes 1052704 | tf_op jit(solution)/shard_map/ppermute | solution.py:515
  245.4 1.5 collective-permute-start.12
  246.9 2.4 merge.11
  249.3 0.6 collective-permute-start.11
  249.9 1.3 collective-permute-start.20
  251.2 1.3 collective-permute-start.17
  253.2 18.7 %collective-permute-done.12.refs_1_ = f32[2056,128]{1,0:T(8,128)} collective-permute-done((f32[2056,128]{1,0:T(8,128)}, f32[2056,128]{1,0:T(8,128)}, u32[]{:S(2)}, u32[]{:S(2)}) %collective-permute-start.12) | collective-permute-done | bytes 1052704 | tf_op jit(solution)/shard_map/ppermute | solution.py:471
  271.9 20.4 %collective-permute-done.11.refs_0_ = f32[2056,128]{1,0:T(8,128)S(1)} collective-permute-done((f32[2056,128]{1,0:T(8,128)}, f32[2056,128]{1,0:T(8,128)S(1)}, u32[]{:S(2)}, u32[]{:S(2)}) %collective-permute-start.11) | collective-permute-done | bytes 1052704 | tf_op jit(solution)/shard_map/ppermute | solution.py:471
  292.3 6.7 %collective-permute-done.17.refs_2_ = f32[2056,128]{1,0:T(8,128)S(1)} collective-permute-done((f32[2056,128]{1,0:T(8,128)}, f32[2056,128]{1,0:T(8,128)S(1)}, u32[]{:S(2)}, u32[]{:S(2)}) %collective-permute-start.17) | collective-permute-done | bytes 1052704 | tf_op jit(solution)/shard_map/ppermute | solution.py:517
  299.0 1.6 copy-done.1
  300.6 1.6 copy-done.2
  302.1 4.3 %final.1 = f32[64,8000]{1,0:T(8,128)} custom-call(s32[1]{0:T(128)} %bitcast.s_ref, f32[1]{0:T(128)} %bitcast.10.mix_ref, f32[64,8000]{1,0:T(8,128)S(1)} %copy-done.1, f32[64,128]{1,0:T(8,128)S(1)} %pad_maximum_fusion.s0_ref, f32[64,128]{1,0:T(8,128)S(1)} %collective-permute-done.s1_ref, f32[64,128]{1,0:T(8,128)S(1)} %collective-permute-done.1.s2_ref, ...), custom_call_target="tpu_custom_call" | custom-call | flops 5000000000 | bytes 12582912 | tf_op jit(solution)/shard_map/final/pallas_call | solution.py:448
  (19 shorter events, 0.1 us)
Async XLA Ops:
  17.5 51.1 %collective-permute-start.4 = (f32[2112,128]{1,0:T(8,128)}, f32[2112,128]{1,0:T(8,128)}, u32[]{:S(2)}, u32[]{:S(2)}) collective-permute-start(f32[2112,128]{1,0:T(8,128)} %get-tuple-element.29), channel_id=1, source_target_pairs={{0,8},{12,4},{1,9},{13,5},{2,10},{14,6},{3,11},{15,7},{16,24},{28,... | collective-permute-start | bytes 3244040 | tf_op jit(solution)/shard_map/ppermute | solution.py:488
  24.5 44.2 %collective-permute-start.5 = (f32[2112,128]{1,0:T(8,128)}, f32[2112,128]{1,0:T(8,128)}, u32[]{:S(2)}, u32[]{:S(2)}) collective-permute-start(f32[2112,128]{1,0:T(8,128)} %get-tuple-element.29), channel_id=1, source_target_pairs={{4,8},{8,4},{5,9},{9,5},{6,10},{10,6},{7,11},{11,7},{20,24},{24,20... | collective-permute-start | bytes 3244040 | tf_op jit(solution)/shard_map/ppermute | solution.py:489
  26.2 45.1 %collective-permute-start.3 = (f32[2112,128]{1,0:T(8,128)}, f32[2112,128]{1,0:T(8,128)}, u32[]{:S(2)}, u32[]{:S(2)}) collective-permute-start(f32[2112,128]{1,0:T(8,128)} %get-tuple-element.28), channel_id=1, source_target_pairs={{0,4},{4,0},{8,12},{12,8},{1,5},{5,1},{9,13},{13,9},{2,6},{6,2},{1... | collective-permute-start | bytes 3244040 | tf_op jit(solution)/shard_map/ppermute | solution.py:490
  43.1 59.1 %collective-permute-start.7 = (f32[2048,128]{1,0:T(8,128)}, f32[2048,128]{1,0:T(8,128)}, u32[]{:S(2)}, u32[]{:S(2)}) collective-permute-start(f32[2048,128]{1,0:T(8,128)} %get-tuple-element.33), channel_id=1, source_target_pairs={{0,8},{12,4},{1,9},{13,5},{2,10},{14,6},{3,11},{15,7},{16,24},{28,... | collective-permute-start | bytes 3145736 | tf_op jit(solution)/shard_map/ppermute | solution.py:492
  47.9 54.3 %collective-permute-start.8 = (f32[2048,128]{1,0:T(8,128)}, f32[2048,128]{1,0:T(8,128)}, u32[]{:S(2)}, u32[]{:S(2)}) collective-permute-start(f32[2048,128]{1,0:T(8,128)} %get-tuple-element.33), channel_id=1, source_target_pairs={{4,8},{8,4},{5,9},{9,5},{6,10},{10,6},{7,11},{11,7},{20,24},{24,20... | collective-permute-start | bytes 3145736 | tf_op jit(solution)/shard_map/ppermute | solution.py:493
  68.7 61.1 %collective-permute-start.14 = (f32[4112,128]{1,0:T(8,128)}, f32[4112,128]{1,0:T(8,128)}, u32[]{:S(2)}, u32[]{:S(2)}) collective-permute-start(f32[4112,128]{1,0:T(8,128)} %get-tuple-element.48), channel_id=1, source_target_pairs={{0,1},{1,0},{2,3},{3,2},{4,5},{5,4},{6,7},{7,6},{8,9},{9,8},{10,11... | collective-permute-start | bytes 6316040 | tf_op jit(solution)/shard_map/ppermute | solution.py:471
  68.8 95.9 %collective-permute-start.13 = (f32[4112,128]{1,0:T(8,128)}, f32[4112,128]{1,0:T(8,128)}, u32[]{:S(2)}, u32[]{:S(2)}) collective-permute-start(f32[4112,128]{1,0:T(8,128)} %get-tuple-element.46), channel_id=1, source_target_pairs={{0,1},{1,0},{2,3},{3,2},{4,5},{5,4},{6,7},{7,6},{8,9},{9,8},{10,11... | collective-permute-start | bytes 6316040 | tf_op jit(solution)/shard_map/ppermute | solution.py:471
  71.3 43.9 %collective-permute-start.6 = (f32[2048,128]{1,0:T(8,128)}, f32[2048,128]{1,0:T(8,128)}, u32[]{:S(2)}, u32[]{:S(2)}) collective-permute-start(f32[2048,128]{1,0:T(8,128)} %get-tuple-element.32), channel_id=1, source_target_pairs={{0,4},{4,0},{8,12},{12,8},{1,5},{5,1},{9,13},{13,9},{2,6},{6,2},{1... | collective-permute-start | bytes 3145736 | tf_op jit(solution)/shard_map/ppermute | solution.py:494
  129.6 74.2 %collective-permute-start.10 = (f32[4112,128]{1,0:T(8,128)}, f32[4112,128]{1,0:T(8,128)}, u32[]{:S(2)}, u32[]{:S(2)}) collective-permute-start(f32[4112,128]{1,0:T(8,128)} %get-tuple-element.43), channel_id=1, source_target_pairs={{0,1},{1,0},{2,3},{3,2},{4,5},{5,4},{6,7},{7,6},{8,9},{9,8},{10,11... | collective-permute-start | bytes 6316040 | tf_op jit(solution)/shard_map/ppermute | solution.py:471
  133.2 33.1 %collective-permute-start.18 = (f32[2056,128]{1,0:T(8,128)}, f32[2056,128]{1,0:T(8,128)}, u32[]{:S(2)}, u32[]{:S(2)}) collective-permute-start(f32[2056,128]{1,0:T(8,128)} %get-tuple-element.50), channel_id=1, source_target_pairs={{0,2},{1,3},{2,0},{3,1},{4,6},{5,7},{6,4},{7,5},{8,10},{9,11},{10,... | collective-permute-start | bytes 3158024 | tf_op jit(solution)/shard_map/ppermute | solution.py:471
  134.8 47.4 %collective-permute-start.15 = (f32[2056,128]{1,0:T(8,128)}, f32[2056,128]{1,0:T(8,128)}, u32[]{:S(2)}, u32[]{:S(2)}) collective-permute-start(f32[2056,128]{1,0:T(8,128)} %get-tuple-element.49), channel_id=1, source_target_pairs={{0,2},{1,3},{2,0},{3,1},{4,6},{5,7},{6,4},{7,5},{8,10},{9,11},{10,... | collective-permute-start | bytes 3158024 | tf_op jit(solution)/shard_map/ppermute | solution.py:471
  163.1 1.3 copy-start
  164.7 84.6 %collective-permute-start = (f32[64,128]{1,0:T(8,128)S(1)}, f32[64,128]{1,0:T(8,128)S(1)}, u32[]{:S(2)}, u32[]{:S(2)}) collective-permute-start(f32[64,128]{1,0:T(8,128)S(1)} %pad_maximum_fusion.s0_ref), channel_id=1, source_target_pairs={{0,1},{1,0},{2,3},{3,2},{4,5},{5,4},{6,7},{7,6},{8,9},{9,8},{10,11... | collective-permute-start | bytes 98312 | tf_op jit(solution)/shard_map/ppermute | solution.py:471
  164.7 85.2 %collective-permute-start.1 = (f32[64,128]{1,0:T(8,128)S(1)}, f32[64,128]{1,0:T(8,128)S(1)}, u32[]{:S(2)}, u32[]{:S(2)}) collective-permute-start(f32[64,128]{1,0:T(8,128)S(1)} %pad_maximum_fusion.s0_ref), channel_id=1, source_target_pairs={{0,2},{1,3},{2,0},{3,1},{4,6},{5,7},{6,4},{7,5},{8,10},{9,11},{10,... | collective-permute-start | bytes 98312 | tf_op jit(solution)/shard_map/ppermute | solution.py:471
  166.3 86.9 %collective-permute-start.9 = (f32[4112,128]{1,0:T(8,128)}, f32[4112,128]{1,0:T(8,128)}, u32[]{:S(2)}, u32[]{:S(2)}) collective-permute-start(f32[4112,128]{1,0:T(8,128)} %get-tuple-element.41), channel_id=1, source_target_pairs={{0,1},{1,0},{2,3},{3,2},{4,5},{5,4},{6,7},{7,6},{8,9},{9,8},{10,11... | collective-permute-start | bytes 6316040 | tf_op jit(solution)/shard_map/ppermute | solution.py:471
  182.1 42.0 %collective-permute-start.19 = (f32[2056,128]{1,0:T(8,128)}, f32[2056,128]{1,0:T(8,128)}, u32[]{:S(2)}, u32[]{:S(2)}) collective-permute-start(f32[2056,128]{1,0:T(8,128)} %merge.12.refs_0_), channel_id=1, source_target_pairs={{0,4},{12,8},{1,5},{13,9},{2,6},{14,10},{3,7},{15,11},{16,20},{28,... | collective-permute-start | bytes 3158024 | tf_op jit(solution)/shard_map/ppermute | solution.py:515
  203.9 41.5 %collective-permute-start.16 = (f32[2056,128]{1,0:T(8,128)}, f32[2056,128]{1,0:T(8,128)}, u32[]{:S(2)}, u32[]{:S(2)}) collective-permute-start(f32[2056,128]{1,0:T(8,128)} %merge.10.refs_0_), channel_id=1, source_target_pairs={{0,4},{12,8},{1,5},{13,9},{2,6},{14,10},{3,7},{15,11},{16,20},{28,... | collective-permute-start | bytes 3158024 | tf_op jit(solution)/shard_map/ppermute | solution.py:515
  224.1 27.1 %collective-permute-start.2 = (f32[64,128]{1,0:T(8,128)S(1)}, f32[64,128]{1,0:T(8,128)S(1)}, u32[]{:S(2)}, u32[]{:S(2)}) collective-permute-start(f32[64,128]{1,0:T(8,128)S(1)} %pad_maximum_fusion.s0_ref), channel_id=1, source_target_pairs={{0,3},{1,2},{2,1},{3,0},{4,7},{5,6},{6,5},{7,4},{8,11},{9,10},{10,... | collective-permute-start | bytes 98312 | tf_op jit(solution)/shard_map/ppermute | solution.py:471
  245.4 26.4 %collective-permute-start.12 = (f32[2056,128]{1,0:T(8,128)}, f32[2056,128]{1,0:T(8,128)}, u32[]{:S(2)}, u32[]{:S(2)}) collective-permute-start(f32[2056,128]{1,0:T(8,128)} %merge.8), channel_id=1, source_target_pairs={{0,2},{1,3},{2,0},{3,1},{4,6},{5,7},{6,4},{7,5},{8,10},{9,11},{10,... | collective-permute-start | bytes 3158024 | tf_op jit(solution)/shard_map/ppermute | solution.py:471
  249.3 43.0 %collective-permute-start.11 = (f32[2056,128]{1,0:T(8,128)}, f32[2056,128]{1,0:T(8,128)S(1)}, u32[]{:S(2)}, u32[]{:S(2)}) collective-permute-start(f32[2056,128]{1,0:T(8,128)} %merge.7), channel_id=1, source_target_pairs={{0,2},{1,3},{2,0},{3,1},{4,6},{5,7},{6,4},{7,5},{8,10},{9,11},{10,... | collective-permute-start | bytes 3158024 | tf_op jit(solution)/shard_map/ppermute | solution.py:471
  249.9 42.3 %collective-permute-start.20 = (f32[2056,128]{1,0:T(8,128)}, f32[2056,128]{1,0:T(8,128)S(1)}, u32[]{:S(2)}, u32[]{:S(2)}) collective-permute-start(f32[2056,128]{1,0:T(8,128)} %merge.13), channel_id=1, source_target_pairs={{4,12},{8,0},{5,13},{9,1},{6,14},{10,2},{7,15},{11,3},{20,28},{24,... | collective-permute-start | bytes 3158024 | tf_op jit(solution)/shard_map/ppermute | solution.py:517
  251.2 47.7 %collective-permute-start.17 = (f32[2056,128]{1,0:T(8,128)}, f32[2056,128]{1,0:T(8,128)S(1)}, u32[]{:S(2)}, u32[]{:S(2)}) collective-permute-start(f32[2056,128]{1,0:T(8,128)} %merge.11), channel_id=1, source_target_pairs={{4,12},{8,0},{5,13},{9,1},{6,14},{10,2},{7,15},{11,3},{20,28},{24,... | collective-permute-start | bytes 3158024 | tf_op jit(solution)/shard_map/ppermute | solution.py:517
  299.0 1.6 copy-start.1
  300.6 1.6 copy-start.2

commit v4 on v3

--- a/solution.py
+++ b/solution.py
@@ -410,14 +410,14 @@
     )(*arrays)
 
 
-def final_kernel(chunks, s_ref, mix_ref, logits_ref, s0_ref, s1_ref, s2_ref, s3_ref, keep_ref, mate_ref, *refs):
-    y_refs, far_refs, out_ref = refs[:chunks], refs[chunks:2 * chunks], refs[2 * chunks]
+def final_kernel(chunks, s_ref, mix_ref, logits_ref, s0_ref, s1_ref, s2_ref, s3_ref, *refs):
+    home_refs, y_refs, far_refs, out_ref = refs[:chunks], refs[chunks:2 * chunks], refs[2 * chunks:3 * chunks], refs[3 * chunks]
     mix = mix_ref[0]
     end = (s_ref[0] == 0) | (s_ref[0] == 3)
     size = PIECE // chunks
-    metas = [r[size:size + META, :] for r in (keep_ref, mate_ref, y_refs[0], far_refs[0])]
+    metas = [r[size:size + META, :] for r in (home_refs[0], y_refs[0], far_refs[0])]
     tops = [t[1:2] for t in metas]
-    tops[3] = jnp.where(end, tops[3], -jnp.inf)
+    tops[2] = jnp.where(end, tops[2], -jnp.inf)
     top = functools.reduce(jnp.maximum, tops)
     scales = [jnp.exp(t - top) for t in tops]
     z = sum(t[0:1] * f for t, f in zip(metas, scales))
@@ -432,8 +432,7 @@
 
     for i in range(0, PIECE, LANES):
         c, at = i // size, i % size
-        base = c * (size + META) + at
-        parts = [keep_ref[base:base + LANES, :], mate_ref[base:base + LANES, :], y_refs[c][at:at + LANES, :], far_refs[c][at:at + LANES, :]]
+        parts = [r[c][at:at + LANES, :] for r in (home_refs, y_refs, far_refs)]
         h = sum(p * f for p, f in zip(parts, scales))
         h = h.T
         out_ref[:, i:i + LANES] = jnp.log(h[:64] + lm(i, LANES))
@@ -442,18 +441,18 @@
             out_ref[:, PIECE + i:PIECE + i + count] = jnp.log(h[64:, :count] + lm(PIECE + i, count))
 
 
-def final_call(s1, mix, logits, stats, keep, mate, from_y, far):
+def final_call(s1, mix, logits, stats, home, from_y, far):
     vmem = pl.BlockSpec(memory_space=pltpu.VMEM)
     smem = pl.BlockSpec(memory_space=pltpu.SMEM)
     return pl.pallas_call(
         functools.partial(final_kernel, len(far)),
-        in_specs=[smem, smem] + [vmem] * (7 + 2 * len(far)),
+        in_specs=[smem, smem] + [vmem] * (5 + 3 * len(far)),
         out_specs=vmem,
         out_shape=jax.ShapeDtypeStruct(logits.shape, jnp.float32),
         compiler_params=pltpu.CompilerParams(vmem_limit_bytes=40 * 1024 * 1024),
         cost_estimate=pl.CostEstimate(flops=5_000_000_000, bytes_accessed=12 << 20, transcendentals=1 << 20),
         name="final",
-    )(s1, mix, logits, *stats, keep, mate, *from_y, *far)
+    )(s1, mix, logits, *stats, *home, *from_y, *far)
 
 
 NEAR = [(0, 1), (1, 0), (2, 3), (3, 2)]
@@ -521,12 +520,13 @@
             part, = merge_call(size, [ynext, matey], [(c, c)])
             from_y.append(swap(part, "model", 2))
 
+        home = merge_call(size, [keep, mate], [(c, c) for c in range(CHUNKS)])
         my_rows = lax.dynamic_slice_in_dim(queries, s * rows_loc, rows_loc, axis=0)
         logits = lax.dot_general(my_rows, w_head, (((1,), (0,)), ((), ())), preferred_element_type=jnp.float32)
         lm_top = jnp.max(logits, axis=1, keepdims=True)
         lm_sum = jnp.sum(jnp.exp(logits - lm_top), axis=1, keepdims=True)
         stats = jnp.concatenate([jnp.broadcast_to(lm_top, (rows_loc, 64)), jnp.broadcast_to(lm_sum, (rows_loc, 64))], axis=1)
         stats = [stats] + [swap(stats, "model", k) for k in (1, 2, 3)]
-        return final_call(s1, mix_weight.reshape(1), logits, stats, keep, mate, from_y, far)
+        return final_call(s1, mix_weight.reshape(1), logits, stats, home, from_y, far)
 
     return jax.shard_map(local_step, mesh=mesh, in_specs=(P("data", None), P(None, "model"), P(("store", "model"), None), P(("store", "model")), P(), P()), out_specs=P(("data", "store"), "model"), check_vma=False)

time: 307 us -> 308 us (level)
  waiting for transfers between devices: 106 us -> 100 us
    ppermute x11, waiting for transfers between devices: 52 us -> 27 us  [swap(): return lax.ppermute(x, axis, [(i, i ^ bit) for i in range(4)])]
    ppermute x2, waiting for transfers between devices: 6.71 us -> 28.1 us  [local_step(): far.append(lax.ppermute(pair, 'store', ACROSS))]
    pallas_call x7 -> x8, Pallas kernels: 18.4 us -> 21.8 us  [merge_call(): pl.pallas_call(functools.partial(merge_kernel, size, tuple((tuple((c * (s...]
  transfers between devices with their start and end apart: 21 -> 21, of which waited for: 8 -> 9; matrix products, arithmetic and copies ran while one was open for 9% -> 9% of each run, Pallas kernels for 32% -> 33%
where the time goes in v4:
time: 308 us; the launch traced here: 307 us
  Pallas kernels  122 us (40%)
  waiting for transfers between devices  100 us (32%)
  starting transfers between devices  49.4 us (16%)
  matrix products  27.4 us (9%)
  local copies, waits for them, and re-layouts  5.48 us (2%)
    pallas_call x3, Pallas kernels, scatter_call(): pl.pallas_call(functools.partial(scatter_kernel, tuple((seg[1:] for seg i...  60.7 us
    pallas_call x2, Pallas kernels, score_call(): pl.pallas_call(functools.partial(scores_kernel, first, count, bool(prev))...  33.8 us
    ppermute x2, waiting for transfers between devices, local_step(): inward = lax.ppermute(plane, 'store', INWARD)  30.3 us
    ppermute x2, waiting for transfers between devices, local_step(): far.append(lax.ppermute(pair, 'store', ACROSS))  28.1 us
    dot_general x1, matrix products, local_step(): lax.dot_general(my_rows, w_head, (((1,), (0,)), ((), ())), preferred_elem...  27.4 us
    ppermute x11, waiting for transfers between devices, swap(): return lax.ppermute(x, axis, [(i, i ^ bit) for i in range(4)])  27 us
    pallas_call x8, Pallas kernels, merge_call(): pl.pallas_call(functools.partial(merge_kernel, size, tuple((tuple((c * (s...  21.8 us
    ppermute x2, starting transfers between devices, local_step(): inward = lax.ppermute(plane, 'store', INWARD)  21.3 us
  transfers between devices with their start and end apart: 21, of which 9 were waited for; matrix products, arithmetic and copies ran while one was open for 9% of the time, Pallas kernels for 33%

profile of v4, /device:TPU:0, one launch (start us, length us, event | category | flops | bytes accessed | tf_op | source)
XLA Modules:
  0.0 306.8 jit_solution(9756232135778486989)
XLA Ops:
  0.7 16.9 %scores.2 = (f32[4096,128]{1,0:T(8,128)}, f32[2112,128]{1,0:T(8,128)}, f32[2112,128]{1,0:T(8,128)}, f32[4096,128]{1,0:T(8,128)}, s32[64,128]{1,0:T(8,128)}) custom-call(s32[1]{0:T(128)} %bitcast.s_ref, s32[1]{0:T(128)} %bitcast.2.m_ref, f32[1]{0:T(128)} %bitcast.8.tau_ref, bf16[256,4096]{1,0:T(8,128)(2,1)} %q_hbm.3, bf16[8192,4096]{1,0:T(8,128)(2,1)} %k_hbm.3, ...), custom_call_target="tpu_custom_call" | custom-call | flops 8589934592 | bytes 33554432 | tf_op jit(solution)/shard_map/scores/pallas_call | solution.py:136
  17.6 7.0 %collective-permute-start.4 = (f32[2112,128]{1,0:T(8,128)}, f32[2112,128]{1,0:T(8,128)}, u32[]{:S(2)}, u32[]{:S(2)}) collective-permute-start(f32[2112,128]{1,0:T(8,128)} %get-tuple-element.31), channel_id=1, source_target_pairs={{0,8},{12,4},{1,9},{13,5},{2,10},{14,6},{3,11},{15,7},{16,24},{28,... | collective-permute-start | bytes 3244040 | tf_op jit(solution)/shard_map/ppermute | solution.py:487
  24.5 1.7 collective-permute-start.5
  26.2 16.9 %scores.3 = (f32[4096,128]{1,0:T(8,128)}, f32[2048,128]{1,0:T(8,128)}, f32[2048,128]{1,0:T(8,128)}, f32[4096,128]{1,0:T(8,128)}) custom-call(s32[1]{0:T(128)} %bitcast.s_ref, s32[1]{0:T(128)} %bitcast.2.m_ref, f32[1]{0:T(128)} %bitcast.9.tau_ref, bf16[256,4096]{1,0:T(8,128)(2,1)} %q_hbm.3, ...), custom_call_target="tpu_custom_call", output_to_operand_aliasing={{0}: (6, {}), {3}: (7, {})} | custom-call | flops 8589934592 | bytes 33554432 | tf_op jit(solution)/shard_map/scores/pallas_call | solution.py:136
  43.1 4.8 %collective-permute-start.7 = (f32[2048,128]{1,0:T(8,128)}, f32[2048,128]{1,0:T(8,128)}, u32[]{:S(2)}, u32[]{:S(2)}) collective-permute-start(f32[2048,128]{1,0:T(8,128)} %get-tuple-element.35), channel_id=1, source_target_pairs={{0,8},{12,4},{1,9},{13,5},{2,10},{14,6},{3,11},{15,7},{16,24},{28,... | collective-permute-start | bytes 3145736 | tf_op jit(solution)/shard_map/ppermute | solution.py:491
  47.9 1.7 collective-permute-start.8
  49.6 19.2 %scatter.5 = (f32[4112,128]{1,0:T(8,128)}, f32[4112,128]{1,0:T(8,128)}, f32[4112,128]{1,0:T(8,128)}, f32[4112,128]{1,0:T(8,128)}) custom-call(s32[1]{0:T(128)} %bitcast.s_ref, s32[8192]{0:T(1024)} %bitcast.15, f32[4096,128]{1,0:T(8,128)} %get-tuple-element.48.refs_1_), custom_call_target="tpu_custom_call" | custom-call | flops 8192000000 | bytes 4194304 | tf_op jit(solution)/shard_map/scatter/pallas_call | solution.py:338
  68.9 0.5 collective-permute-start.13
  69.4 1.9 collective-permute-done.3.refs_0_.refs_3_
  71.3 2.5 collective-permute-start.6
  73.8 1.5 ids.1
  75.2 27.0 %scatter.3 = (f32[4112,128]{1,0:T(8,128)}, f32[4112,128]{1,0:T(8,128)}, f32[4112,128]{1,0:T(8,128)}, f32[4112,128]{1,0:T(8,128)}) custom-call(s32[1]{0:T(128)} %bitcast.s_ref, s32[8192]{0:T(1024)} %bitcast.16, s32[24576]{0:T(1024)} %bitcast.13, f32[4096,128]{1,0:T(8,128)} %get-tuple-element.37.refs_2_, f32[2112,128]{1,0:T(8,128)} %collective-permute-done.3.refs_0_.refs_3_, ...), custom_call_target="tpu_custom_call" | custom-call | flops 20480000000 | bytes 10485760 | tf_op jit(solution)/shard_map/scatter/pallas_call | solution.py:338
  102.3 12.9 %collective-permute-done.6.refs_1_ = f32[2048,128]{1,0:T(8,128)} collective-permute-done((f32[2048,128]{1,0:T(8,128)}, f32[2048,128]{1,0:T(8,128)}, u32[]{:S(2)}, u32[]{:S(2)}) %collective-permute-start.6) | collective-permute-done | bytes 1048608 | tf_op jit(solution)/shard_map/ppermute | solution.py:493
  115.1 14.5 %scatter.4 = (f32[4112,128]{1,0:T(8,128)}, f32[4112,128]{1,0:T(8,128)}, f32[4112,128]{1,0:T(8,128)}, f32[4112,128]{1,0:T(8,128)}) custom-call(s32[1]{0:T(128)} %bitcast.s_ref, s32[24576]{0:T(1024)} %bitcast.14, f32[2048,128]{1,0:T(8,128)} %collective-permute-done.6.refs_1_, f32[2048,128]{1,0:T(8,128)} %collective-permute-done.7.refs_2_, ...), custom_call_target="tpu_custom_call" | custom-call | flops 12288000000 | bytes 6291456 | tf_op jit(solution)/shard_map/scatter/pallas_call | solution.py:338
  129.7 0.1 collective-permute-start.10
  129.8 3.4 %merge.11 = (f32[2056,128]{1,0:T(8,128)}, f32[2056,128]{1,0:T(8,128)}) custom-call(f32[4112,128]{1,0:T(8,128)} %get-tuple-element.51.refs_0_, f32[4112,128]{1,0:T(8,128)} %collective-permute-done.14.refs_1_), custom_call_target="tpu_custom_call" | custom-call | flops 4000000000 | bytes 8388608 | tf_op jit(solution)/shard_map/merge/pallas_call | solution.py:399
  133.2 1.6 collective-permute-start.18
  134.8 0.5 collective-permute-start.15
  135.3 27.4 %fusion.3 = (f32[64]{0:T(128)S(1)}, f32[64,8000]{1,0:T(8,128)S(1)}) fusion(bf16[4096,8000]{0,1:T(8,128)(2,1)} %param.7, bf16[256,4096]{1,0:T(8,128)(2,1)} %q_hbm.3, s32[]{:T(128)S(6)} %select_n.3), kind=kOutput, calls=%fused_computation.5 | convolution fusion | flops 4194816000 | bytes 68108544 | tf_op jit(solution)/shard_map/dot_general | solution.py:525
  162.6 0.5 exponential_reduce_fusion
  163.1 1.3 copy-done
  164.6 0.1 pad_maximum_fusion.s0_ref
  164.7 1.6 collective-permute-start.1
  166.3 0.1 collective-permute-start.9
  166.4 2.7 merge.14.refs_0_
  169.2 12.9 %collective-permute-done.15.refs_2_ = f32[2056,128]{1,0:T(8,128)} collective-permute-done((f32[2056,128]{1,0:T(8,128)}, f32[2056,128]{1,0:T(8,128)}, u32[]{:S(2)}, u32[]{:S(2)}) %collective-permute-start.15) | collective-permute-done | bytes 1052704 | tf_op jit(solution)/shard_map/ppermute | solution.py:470
  182.1 19.0 %collective-permute-start.19 = (f32[2056,128]{1,0:T(8,128)}, f32[2056,128]{1,0:T(8,128)}, u32[]{:S(2)}, u32[]{:S(2)}) collective-permute-start(f32[2056,128]{1,0:T(8,128)} %merge.14.refs_0_), channel_id=1, source_target_pairs={{0,4},{12,8},{1,5},{13,9},{2,6},{14,10},{3,7},{15,11},{16,20},{28,... | collective-permute-start | bytes 3158024 | tf_op jit(solution)/shard_map/ppermute | solution.py:514
  201.1 2.8 merge.12.refs_0_
  203.9 2.3 collective-permute-start.16
  206.2 2.4 merge.10
  208.6 2.4 merge.9
  210.9 13.2 %collective-permute-done.19.refs_1_ = f32[2056,128]{1,0:T(8,128)} collective-permute-done((f32[2056,128]{1,0:T(8,128)}, f32[2056,128]{1,0:T(8,128)}, u32[]{:S(2)}, u32[]{:S(2)}) %collective-permute-start.19) | collective-permute-done | bytes 1052704 | tf_op jit(solution)/shard_map/ppermute | solution.py:514
  224.1 1.9 collective-permute-start.12
  226.0 2.4 merge.15
  228.4 17.1 %collective-permute-done.16.refs_1_ = f32[2056,128]{1,0:T(8,128)} collective-permute-done((f32[2056,128]{1,0:T(8,128)}, f32[2056,128]{1,0:T(8,128)}, u32[]{:S(2)}, u32[]{:S(2)}) %collective-permute-start.16) | collective-permute-done | bytes 1052704 | tf_op jit(solution)/shard_map/ppermute | solution.py:514
  245.5 1.5 collective-permute-start.11
  246.9 2.4 merge.13
  249.3 1.3 collective-permute-start.20
  250.6 1.3 collective-permute-start.17
  252.6 3.4 %merge.8 = (f32[2056,128]{1,0:T(8,128)}, f32[2056,128]{1,0:T(8,128)}) custom-call(f32[4112,128]{1,0:T(8,128)} %get-tuple-element.42.refs_0_, f32[4112,128]{1,0:T(8,128)} %collective-permute-done.9.refs_1_), custom_call_target="tpu_custom_call" | custom-call | flops 4000000000 | bytes 8388608 | tf_op jit(solution)/shard_map/merge/pallas_call | solution.py:399
  256.1 12.9 %collective-permute-done.2.s3_ref = f32[64,128]{1,0:T(8,128)S(1)} collective-permute-done((f32[64,128]{1,0:T(8,128)S(1)}, f32[64,128]{1,0:T(8,128)S(1)}, u32[]{:S(2)}, u32[]{:S(2)}) %collective-permute-start.2) | collective-permute-done | bytes 32800 | tf_op jit(solution)/shard_map/ppermute | solution.py:470
  268.9 1.2 collective-permute-done.11.refs_2_
  270.2 8.4 %collective-permute-done.20.refs_5_ = f32[2056,128]{1,0:T(8,128)} collective-permute-done((f32[2056,128]{1,0:T(8,128)}, f32[2056,128]{1,0:T(8,128)}, u32[]{:S(2)}, u32[]{:S(2)}) %collective-permute-start.20) | collective-permute-done | bytes 1052704 | tf_op jit(solution)/shard_map/ppermute | solution.py:516
  278.5 19.8 %collective-permute-done.17.refs_4_ = f32[2056,128]{1,0:T(8,128)} collective-permute-done((f32[2056,128]{1,0:T(8,128)}, f32[2056,128]{1,0:T(8,128)}, u32[]{:S(2)}, u32[]{:S(2)}) %collective-permute-start.17) | collective-permute-done | bytes 1052704 | tf_op jit(solution)/shard_map/ppermute | solution.py:516
  298.3 1.6 copy-done.1
  299.9 1.2 copy-done.2
  301.1 1.2 copy-done.3
  302.3 4.4 %final.1 = f32[64,8000]{1,0:T(8,128)} custom-call(s32[1]{0:T(128)} %bitcast.s_ref, f32[1]{0:T(128)} %bitcast.10.mix_ref, f32[64,8000]{1,0:T(8,128)S(1)} %copy-done.1, f32[64,128]{1,0:T(8,128)S(1)} %pad_maximum_fusion.s0_ref, f32[64,128]{1,0:T(8,128)S(1)} %collective-permute-done.s1_ref, f32[64,128]{1,0:T(8,128)S(1)} %collective-permute-done.1.s2_ref, ...), custom_call_target="tpu_custom_call" | custom-call | flops 5000000000 | bytes 12582912 | tf_op jit(solution)/shard_map/final/pallas_call | solution.py:447
  (22 shorter events, 0.3 us)
Async XLA Ops:
  17.6 51.2 %collective-permute-start.4 = (f32[2112,128]{1,0:T(8,128)}, f32[2112,128]{1,0:T(8,128)}, u32[]{:S(2)}, u32[]{:S(2)}) collective-permute-start(f32[2112,128]{1,0:T(8,128)} %get-tuple-element.31), channel_id=1, source_target_pairs={{0,8},{12,4},{1,9},{13,5},{2,10},{14,6},{3,11},{15,7},{16,24},{28,... | collective-permute-start | bytes 3244040 | tf_op jit(solution)/shard_map/ppermute | solution.py:487
  24.5 44.4 %collective-permute-start.5 = (f32[2112,128]{1,0:T(8,128)}, f32[2112,128]{1,0:T(8,128)}, u32[]{:S(2)}, u32[]{:S(2)}) collective-permute-start(f32[2112,128]{1,0:T(8,128)} %get-tuple-element.31), channel_id=1, source_target_pairs={{4,8},{8,4},{5,9},{9,5},{6,10},{10,6},{7,11},{11,7},{20,24},{24,20... | collective-permute-start | bytes 3244040 | tf_op jit(solution)/shard_map/ppermute | solution.py:488
  26.2 45.1 %collective-permute-start.3 = (f32[2112,128]{1,0:T(8,128)}, f32[2112,128]{1,0:T(8,128)}, u32[]{:S(2)}, u32[]{:S(2)}) collective-permute-start(f32[2112,128]{1,0:T(8,128)} %get-tuple-element.30), channel_id=1, source_target_pairs={{0,4},{4,0},{8,12},{12,8},{1,5},{5,1},{9,13},{13,9},{2,6},{6,2},{1... | collective-permute-start | bytes 3244040 | tf_op jit(solution)/shard_map/ppermute | solution.py:489
  43.1 59.2 %collective-permute-start.7 = (f32[2048,128]{1,0:T(8,128)}, f32[2048,128]{1,0:T(8,128)}, u32[]{:S(2)}, u32[]{:S(2)}) collective-permute-start(f32[2048,128]{1,0:T(8,128)} %get-tuple-element.35), channel_id=1, source_target_pairs={{0,8},{12,4},{1,9},{13,5},{2,10},{14,6},{3,11},{15,7},{16,24},{28,... | collective-permute-start | bytes 3145736 | tf_op jit(solution)/shard_map/ppermute | solution.py:491
  47.9 54.4 %collective-permute-start.8 = (f32[2048,128]{1,0:T(8,128)}, f32[2048,128]{1,0:T(8,128)}, u32[]{:S(2)}, u32[]{:S(2)}) collective-permute-start(f32[2048,128]{1,0:T(8,128)} %get-tuple-element.35), channel_id=1, source_target_pairs={{4,8},{8,4},{5,9},{9,5},{6,10},{10,6},{7,11},{11,7},{20,24},{24,20... | collective-permute-start | bytes 3145736 | tf_op jit(solution)/shard_map/ppermute | solution.py:492
  68.8 61.0 %collective-permute-start.14 = (f32[4112,128]{1,0:T(8,128)}, f32[4112,128]{1,0:T(8,128)}, u32[]{:S(2)}, u32[]{:S(2)}) collective-permute-start(f32[4112,128]{1,0:T(8,128)} %get-tuple-element.52), channel_id=1, source_target_pairs={{0,1},{1,0},{2,3},{3,2},{4,5},{5,4},{6,7},{7,6},{8,9},{9,8},{10,11... | collective-permute-start | bytes 6316040 | tf_op jit(solution)/shard_map/ppermute | solution.py:470
  68.9 95.8 %collective-permute-start.13 = (f32[4112,128]{1,0:T(8,128)}, f32[4112,128]{1,0:T(8,128)}, u32[]{:S(2)}, u32[]{:S(2)}) collective-permute-start(f32[4112,128]{1,0:T(8,128)} %get-tuple-element.50), channel_id=1, source_target_pairs={{0,1},{1,0},{2,3},{3,2},{4,5},{5,4},{6,7},{7,6},{8,9},{9,8},{10,11... | collective-permute-start | bytes 6316040 | tf_op jit(solution)/shard_map/ppermute | solution.py:470
  71.3 43.9 %collective-permute-start.6 = (f32[2048,128]{1,0:T(8,128)}, f32[2048,128]{1,0:T(8,128)}, u32[]{:S(2)}, u32[]{:S(2)}) collective-permute-start(f32[2048,128]{1,0:T(8,128)} %get-tuple-element.34), channel_id=1, source_target_pairs={{0,4},{4,0},{8,12},{12,8},{1,5},{5,1},{9,13},{13,9},{2,6},{6,2},{1... | collective-permute-start | bytes 3145736 | tf_op jit(solution)/shard_map/ppermute | solution.py:493
  129.7 74.2 %collective-permute-start.10 = (f32[4112,128]{1,0:T(8,128)}, f32[4112,128]{1,0:T(8,128)}, u32[]{:S(2)}, u32[]{:S(2)}) collective-permute-start(f32[4112,128]{1,0:T(8,128)} %get-tuple-element.47), channel_id=1, source_target_pairs={{0,1},{1,0},{2,3},{3,2},{4,5},{5,4},{6,7},{7,6},{8,9},{9,8},{10,11... | collective-permute-start | bytes 6316040 | tf_op jit(solution)/shard_map/ppermute | solution.py:470
  133.2 33.1 %collective-permute-start.18 = (f32[2056,128]{1,0:T(8,128)}, f32[2056,128]{1,0:T(8,128)}, u32[]{:S(2)}, u32[]{:S(2)}) collective-permute-start(f32[2056,128]{1,0:T(8,128)} %get-tuple-element.54), channel_id=1, source_target_pairs={{0,2},{1,3},{2,0},{3,1},{4,6},{5,7},{6,4},{7,5},{8,10},{9,11},{10,... | collective-permute-start | bytes 3158024 | tf_op jit(solution)/shard_map/ppermute | solution.py:470
  134.8 47.4 %collective-permute-start.15 = (f32[2056,128]{1,0:T(8,128)}, f32[2056,128]{1,0:T(8,128)}, u32[]{:S(2)}, u32[]{:S(2)}) collective-permute-start(f32[2056,128]{1,0:T(8,128)} %get-tuple-element.53), channel_id=1, source_target_pairs={{0,2},{1,3},{2,0},{3,1},{4,6},{5,7},{6,4},{7,5},{8,10},{9,11},{10,... | collective-permute-start | bytes 3158024 | tf_op jit(solution)/shard_map/ppermute | solution.py:470
  163.1 1.3 copy-start
  164.7 84.6 %collective-permute-start = (f32[64,128]{1,0:T(8,128)S(1)}, f32[64,128]{1,0:T(8,128)S(1)}, u32[]{:S(2)}, u32[]{:S(2)}) collective-permute-start(f32[64,128]{1,0:T(8,128)S(1)} %pad_maximum_fusion.s0_ref), channel_id=1, source_target_pairs={{0,1},{1,0},{2,3},{3,2},{4,5},{5,4},{6,7},{7,6},{8,9},{9,8},{10,11... | collective-permute-start | bytes 98312 | tf_op jit(solution)/shard_map/ppermute | solution.py:470
  164.7 85.9 %collective-permute-start.1 = (f32[64,128]{1,0:T(8,128)S(1)}, f32[64,128]{1,0:T(8,128)S(1)}, u32[]{:S(2)}, u32[]{:S(2)}) collective-permute-start(f32[64,128]{1,0:T(8,128)S(1)} %pad_maximum_fusion.s0_ref), channel_id=1, source_target_pairs={{0,2},{1,3},{2,0},{3,1},{4,6},{5,7},{6,4},{7,5},{8,10},{9,11},{10,... | collective-permute-start | bytes 98312 | tf_op jit(solution)/shard_map/ppermute | solution.py:470
  166.3 86.3 %collective-permute-start.9 = (f32[4112,128]{1,0:T(8,128)}, f32[4112,128]{1,0:T(8,128)}, u32[]{:S(2)}, u32[]{:S(2)}) collective-permute-start(f32[4112,128]{1,0:T(8,128)} %get-tuple-element.43), channel_id=1, source_target_pairs={{0,1},{1,0},{2,3},{3,2},{4,5},{5,4},{6,7},{7,6},{8,9},{9,8},{10,11... | collective-permute-start | bytes 6316040 | tf_op jit(solution)/shard_map/ppermute | solution.py:470
  182.1 42.0 %collective-permute-start.19 = (f32[2056,128]{1,0:T(8,128)}, f32[2056,128]{1,0:T(8,128)}, u32[]{:S(2)}, u32[]{:S(2)}) collective-permute-start(f32[2056,128]{1,0:T(8,128)} %merge.14.refs_0_), channel_id=1, source_target_pairs={{0,4},{12,8},{1,5},{13,9},{2,6},{14,10},{3,7},{15,11},{16,20},{28,... | collective-permute-start | bytes 3158024 | tf_op jit(solution)/shard_map/ppermute | solution.py:514
  203.9 41.5 %collective-permute-start.16 = (f32[2056,128]{1,0:T(8,128)}, f32[2056,128]{1,0:T(8,128)}, u32[]{:S(2)}, u32[]{:S(2)}) collective-permute-start(f32[2056,128]{1,0:T(8,128)} %merge.12.refs_0_), channel_id=1, source_target_pairs={{0,4},{12,8},{1,5},{13,9},{2,6},{14,10},{3,7},{15,11},{16,20},{28,... | collective-permute-start | bytes 3158024 | tf_op jit(solution)/shard_map/ppermute | solution.py:514
  224.1 44.8 %collective-permute-start.12 = (f32[2056,128]{1,0:T(8,128)}, f32[2056,128]{1,0:T(8,128)}, u32[]{:S(2)}, u32[]{:S(2)}) collective-permute-start(f32[2056,128]{1,0:T(8,128)} %merge.10), channel_id=1, source_target_pairs={{0,2},{1,3},{2,0},{3,1},{4,6},{5,7},{6,4},{7,5},{8,10},{9,11},{10,... | collective-permute-start | bytes 3158024 | tf_op jit(solution)/shard_map/ppermute | solution.py:470
  245.5 24.7 %collective-permute-start.11 = (f32[2056,128]{1,0:T(8,128)}, f32[2056,128]{1,0:T(8,128)}, u32[]{:S(2)}, u32[]{:S(2)}) collective-permute-start(f32[2056,128]{1,0:T(8,128)} %merge.9), channel_id=1, source_target_pairs={{0,2},{1,3},{2,0},{3,1},{4,6},{5,7},{6,4},{7,5},{8,10},{9,11},{10,... | collective-permute-start | bytes 3158024 | tf_op jit(solution)/shard_map/ppermute | solution.py:470
  249.3 29.2 %collective-permute-start.20 = (f32[2056,128]{1,0:T(8,128)}, f32[2056,128]{1,0:T(8,128)}, u32[]{:S(2)}, u32[]{:S(2)}) collective-permute-start(f32[2056,128]{1,0:T(8,128)} %merge.15), channel_id=1, source_target_pairs={{4,12},{8,0},{5,13},{9,1},{6,14},{10,2},{7,15},{11,3},{20,28},{24,... | collective-permute-start | bytes 3158024 | tf_op jit(solution)/shard_map/ppermute | solution.py:516
  250.6 47.7 %collective-permute-start.17 = (f32[2056,128]{1,0:T(8,128)}, f32[2056,128]{1,0:T(8,128)}, u32[]{:S(2)}, u32[]{:S(2)}) collective-permute-start(f32[2056,128]{1,0:T(8,128)} %merge.13), channel_id=1, source_target_pairs={{4,12},{8,0},{5,13},{9,1},{6,14},{10,2},{7,15},{11,3},{20,28},{24,... | collective-permute-start | bytes 3158024 | tf_op jit(solution)/shard_map/ppermute | solution.py:516
  252.6 16.4 %collective-permute-start.2 = (f32[64,128]{1,0:T(8,128)S(1)}, f32[64,128]{1,0:T(8,128)S(1)}, u32[]{:S(2)}, u32[]{:S(2)}) collective-permute-start(f32[64,128]{1,0:T(8,128)S(1)} %pad_maximum_fusion.s0_ref), channel_id=1, source_target_pairs={{0,3},{1,2},{2,1},{3,0},{4,7},{5,6},{6,5},{7,4},{8,11},{9,10},{10,... | collective-permute-start | bytes 98312 | tf_op jit(solution)/shard_map/ppermute | solution.py:470
  298.3 1.6 copy-start.1
  299.9 1.2 copy-start.2
  301.1 1.2 copy-start.3
